TPU v7x, 512 devices: a 4x2x32 block of a 4x8x32 slice. The times are simulated.
512 devices in a mesh: angle: 2 (over y), row: 128 (over z, x), col: 2 (over core).
Axes of the slice: x: 4, y: 2, z: 32, core: 2. Of those that a mesh axis runs over, the one named last changes fastest.
The devices are a block of a 4x8x32 slice.
Arguments:
- obj_field: float32 [2, 32768, 1024], P(None, ('angle', 'row'), 'col'), parts along dimension 1, may hold values from -6 to 6
- probe_modes: bfloat16 [2, 6, 256, 256], replicated, may hold values from -6 to 6
- centers: int32 [512, 2], P(('angle', 'row', 'col')), parts along dimension 0, may hold values from 0 to 16383, as said below
- amplitudes: float32 [512, 256, 256], P(('angle', 'row', 'col')), parts along dimension 0, may hold values from 0.2 to 4
Outputs:
- new_object: float32 [2, 32768, 1024], P(None, ('angle', 'row'), 'col'), parts along dimension 1
- new_probe: float32 [2, 12, 256, 256], P(None, 'angle'), parts along dimension 1
There are 2 independent parts, one for each index of `angle`. A program takes and returns all parts, laid end to end along the dimension named above; an argument that names none is the same for every part. Nothing has to cross between parts.
Inputs may be any that keep to these rules, and one draw needn't show every extreme that they name: `centers`: position k belongs to device d = k // 1 of the row+col order (row slowest); its centre lies in that device's tile: row in [(d // (1024 // 512)) * 128, + 128), column in [(d % (1024 // 512)) * 512, + 512).
All inputs are finite; a program needn't handle non-finite values.
Results may differ from a plain program's by a relative error of at most 0.0003.
Values sent between devices are 32-bit elements; how exact they have to be, the bound alone decides.
A program may use at most 64 MiB of HBM per device.

v0:
```python
import functools
import math

import jax
import jax.numpy as jnp
from jax import lax
from jax.sharding import Mesh
from jax.sharding import PartitionSpec as P

ROW = ("row_0", "row_1")
ROW_COL = ("row_0", "row_1", "col")
ANGLE_ROW = ("angle", "row_0", "row_1")
ANGLE_ROW_COL = ("angle", "row_0", "row_1", "col")


HIGHEST = lax.Precision.HIGHEST


def padded(block, sides, width):
    for axis, dim in sides:
        count = lax.axis_size(axis)
        forward = [(i, i + 1) for i in range(count - 1)]
        backward = [(target, source) for source, target in forward]
        low = lax.ppermute(
            lax.slice_in_dim(block, block.shape[dim] - width, None, axis=dim), axis, forward
        )
        high = lax.ppermute(lax.slice_in_dim(block, 0, width, axis=dim), axis, backward)
        block = jnp.concatenate([low, block, high], axis=dim)
    return block


def one_axis_at_a_time(x, axes):
    return functools.reduce(lax.pmax, axes, x)


def dft_tables(probe_side):
    indices = jnp.arange(probe_side, dtype=jnp.int32)
    products = indices[:, None] * indices[None, :] % probe_side
    phases = products.astype(jnp.float32) * (2.0 * math.pi / probe_side)
    scaling = 1.0 / math.sqrt(probe_side)
    return (jnp.cos(phases) * scaling, jnp.sin(phases) * scaling)


def transform(in_real, in_imag, cosine_table, sine_table, direction):
    left_real = jnp.einsum(
        "kn,mnv->mkv", cosine_table, in_real, precision=HIGHEST
    ) - direction * jnp.einsum("kn,mnv->mkv", sine_table, in_imag, precision=HIGHEST)
    left_imag = jnp.einsum(
        "kn,mnv->mkv", cosine_table, in_imag, precision=HIGHEST
    ) + direction * jnp.einsum("kn,mnv->mkv", sine_table, in_real, precision=HIGHEST)
    out_real = jnp.einsum(
        "mkv,lv->mkl", left_real, cosine_table, precision=HIGHEST
    ) - direction * jnp.einsum("mkv,lv->mkl", left_imag, sine_table, precision=HIGHEST)
    out_imag = jnp.einsum(
        "mkv,lv->mkl", left_imag, cosine_table, precision=HIGHEST
    ) + direction * jnp.einsum("mkv,lv->mkl", left_real, sine_table, precision=HIGHEST)
    return (out_real, out_imag)


def fold_rows(buffer, margin, interior):
    top_rim = buffer[:, :margin]
    bottom = buffer[:, margin + interior :]
    middle = buffer[:, margin : margin + interior]
    rim_pair = jnp.concatenate([top_rim, bottom], axis=1)
    received = padded(rim_pair, ((ROW, 1),), margin)
    middle = middle.at[:, :margin].add(received[:, :margin])
    middle = middle.at[:, interior - margin :].add(received[:, 3 * margin :])
    return middle


def fold_cols(buffer, margin, interior):
    left_rim = buffer[:, :, :margin]
    right_rim = buffer[:, :, margin + interior :]
    middle = buffer[:, :, margin : margin + interior]
    rim_pair = jnp.concatenate([left_rim, right_rim], axis=2)
    received = padded(rim_pair, (("col", 2),), margin)
    middle = middle.at[:, :, :margin].add(received[:, :, :margin])
    middle = middle.at[:, :, interior - margin :].add(received[:, :, 3 * margin :])
    return middle


def local(obj_field, probe_modes, centers, amplitudes):
    tile_rows = obj_field.shape[1]
    tile_cols = obj_field.shape[2]
    mode_count = probe_modes.shape[1]
    probe_side = probe_modes.shape[2]
    margin = probe_side // 2
    local_count = centers.shape[0]
    row_index = lax.axis_index(ROW)
    col_index = lax.axis_index("col")
    row_anchor = row_index * tile_rows
    col_anchor = col_index * tile_cols
    probe = probe_modes.astype(jnp.float32)
    probe_real = probe[0]
    probe_imag = probe[1]
    spot_map = jnp.sum(probe_real * probe_real + probe_imag * probe_imag, axis=0)
    cosine_table, sine_table = dft_tables(probe_side)
    extended = padded(obj_field, ((ROW, 1), ("col", 2)), margin)
    channels = 3
    illumination = None
    anchor = jnp.zeros((), jnp.int32)

    def visit_position(position, totals):
        buffer, probe_grad, probe_weight = totals
        start_row = centers[position, 0] - row_anchor
        start_col = centers[position, 1] - col_anchor
        window = lax.dynamic_slice(
            extended, (anchor, start_row, start_col), (2, probe_side, probe_side)
        )
        win_real = window[0]
        win_imag = window[1]
        exit_real = probe_real * win_real - probe_imag * win_imag
        exit_imag = probe_real * win_imag + probe_imag * win_real
        far_real, far_imag = transform(exit_real, exit_imag, cosine_table, sine_table, -1.0)
        modulus = jnp.sqrt(jnp.sum(far_real * far_real + far_imag * far_imag, axis=0))
        factor = amplitudes[position] / (modulus + 0.5)
        back_real, back_imag = transform(
            far_real * factor, far_imag * factor, cosine_table, sine_table, 1.0
        )
        diff_real = back_real - exit_real
        diff_imag = back_imag - exit_imag
        obj_real = jnp.sum(probe_real * diff_real + probe_imag * diff_imag, axis=0)
        obj_imag = jnp.sum(probe_real * diff_imag - probe_imag * diff_real, axis=0)
        stacked = jnp.stack([obj_real, obj_imag, spot_map])
        current = lax.dynamic_slice(
            buffer, (anchor, start_row, start_col), (channels, probe_side, probe_side)
        )
        buffer = lax.dynamic_update_slice(buffer, current + stacked, (anchor, start_row, start_col))
        probe_grad = probe_grad + jnp.stack(
            [
                win_real * diff_real + win_imag * diff_imag,
                win_real * diff_imag - win_imag * diff_real,
            ]
        )
        probe_weight = probe_weight + win_real * win_real + win_imag * win_imag
        return (buffer, probe_grad, probe_weight)

    start_state = (
        jnp.zeros((channels, tile_rows + 2 * margin, tile_cols + 2 * margin), jnp.float32),
        jnp.zeros((2, mode_count, probe_side, probe_side), jnp.float32),
        jnp.zeros((probe_side, probe_side), jnp.float32),
    )
    buffer, probe_grad, probe_weight = lax.fori_loop(0, local_count, visit_position, start_state)
    folded = fold_cols(fold_rows(buffer, margin, tile_rows), margin, tile_cols)
    illumination = folded[2]
    numerator = folded[:2]
    peak_value = one_axis_at_a_time(jnp.max(illumination), ROW_COL)
    new_object = obj_field + numerator / (illumination + 0.1 * peak_value)
    grad_sum, weight_sum = lax.psum((probe_grad, probe_weight), ROW_COL)
    peak_weight = jnp.max(weight_sum)
    new_probe = probe + grad_sum / (weight_sum + 0.1 * peak_weight)
    return (new_object, new_probe)


def solution(mesh):
    split = Mesh(
        mesh.devices.reshape(mesh.shape["angle"], 32, 4, mesh.shape["col"]),
        ("angle", "row_0", "row_1", "col"),
    )
    return jax.shard_map(
        local,
        mesh=split,
        in_specs=(
            P(None, ANGLE_ROW, "col"),
            P(),
            P(ANGLE_ROW_COL, None),
            P(ANGLE_ROW_COL, None, None),
        ),
        out_specs=(P(None, ANGLE_ROW, "col"), P(None, "angle", None, None)),
        check_vma=False,
    )
```

profile of v0, /device:TPU:33, one launch (start us, length us, event | category | flops | bytes accessed | tf_op | source)
XLA Modules:
  0.0 833.8 jit_solution(12491875644812034926)
XLA Ops:
  7.2 0.1 all-reduce.3.cloned.1.call-start
  7.2 4.1 collective-permute-start
  11.4 1.3 collective-permute-start.1
  12.7 5.1 collective-permute-done
  17.8 1.1 constant_dynamic-update-slice_fusion.1
  18.9 0.0 copy-start.8
  18.9 2.6 collective-permute-done.1
  21.6 0.0 copy-start.3
  21.6 1.1 copy-done.3
  22.7 0.8 fusion.146
  23.5 42.5 %collective-permute-start.3 = (f32[2,384,128]{2,1,0:T(8,128)}, f32[2,384,128]{2,1,0:T(8,128)}, u32[]{:S(2)}, u32[]{:S(2)}) collective-permute-start(f32[2,384,128]{2,1,0:T(8,128)} %get-tuple-element.125), channel_id=1, source_target_pairs={{1,0},{3,2},{5,4},{7,6},{9,8},{11,10},{13,12},{15,14},{17,16},{19,... | collective-permute-start | bytes 1179656 | tf_op jit(solution)/shard_map/ppermute | solution.py:27
  66.0 1.3 collective-permute-start.2
  67.3 0.6 fusion.148
  69.1 1.7 convert_element_type.36
  70.8 1.6 fusion.36
  72.4 0.0 copy-start.4
  72.5 0.7 copy-done.4
  73.2 0.3 multiply_subtract_fusion.2
  73.5 3.5 fusion.58
  77.1 3.6 fusion.55
  80.7 3.6 multiply_add_fusion.1
  84.3 3.7 fusion.8
  88.0 3.6 fusion.10
  91.6 3.7 multiply_subtract_fusion.1
  95.2 3.8 multiply_subtract_fusion
  99.0 0.0 copy-start.7
  99.0 3.8 add_reduce_fusion.2
  102.9 0.1 fusion.41
  103.0 3.6 fusion.28
  106.6 4.0 fusion.24
  110.6 3.6 convolution_add_fusion
  114.2 3.6 fusion
  117.8 3.6 fusion.2
  121.4 3.7 convolution_subtract_fusion
  125.1 3.6 add_subtract_fusion
  128.7 7.8 add_bitcast_fusion
  136.5 1.0 pad_maximum_fusion.1
  137.4 0.3 broadcast_in_dim.3
  137.7 10.7 %dynamic_update_slice.4 = f32[3,384,768]{2,1,0:T(8,128)S(1)} dynamic-update-slice(f32[3,384,768]{2,1,0:T(8,128)S(1)} %broadcast_in_dim.3, f32[3,256,256]{2,1,0:T(8,128)} %pad_maximum_fusion.1, s32[]{:T(128)} %constant.170.clone.1, s32[]{:T(128)S(6)} %select_n.53, s32[]{:T(128)S(6)} %select_n.54) | dynamic-update-slice | bytes 1572868 | tf_op jit(solution)/shard_map/while/body/eval_jaxpr/dynamic_update_slice | solution.py:128
  148.4 0.0 copy-start
  148.5 1.6 fusion.145
  150.1 3.2 collective-permute-start.4
  153.2 1.3 collective-permute-start.5
  154.6 0.0 copy-start.5
  154.6 2.1 pad_maximum_fusion
  156.6 0.8 multiply_add_fusion.3
  157.4 0.1 all-reduce.3.cloned.1.call-update
  157.5 19.3 %collective-permute-done.4 = f32[3,128,768]{2,1,0:T(8,128)} collective-permute-done((f32[3,128,768]{2,1,0:T(8,128)}, f32[3,128,768]{2,1,0:T(8,128)}, u32[]{:S(2)}, u32[]{:S(2)}) %collective-permute-start.4) | collective-permute-done | bytes 1179680 | tf_op jit(solution)/shard_map/ppermute | solution.py:24
  176.7 4.9 collective-permute-done.5
  181.7 1.8 fusion.30
  183.6 1.4 collective-permute-start.6
  185.0 0.1 slice.158
  185.1 4.4 collective-permute-start.7
  189.6 1.0 collective-permute-done.7
  190.6 0.7 slice_reduce_fusion
  191.3 53.2 %pmax.21 = f32[]{:T(128)} all-reduce(f32[]{:T(128)} %slice_reduce_fusion), channel_id=1, replica_groups=mesh['angle'=2,'row_0'=32,'row_1'=4,'col'=2] {'row_0'}, use_global_device_ids=true, to_apply=%region_5.6 | all-reduce | flops 1 | bytes 8 | tf_op jit(solution)/shard_map/pmax | solution.py:33
  244.5 10.2 %pmax.22 = f32[]{:T(128)} all-reduce(f32[]{:T(128)} %pmax.21), channel_id=1, replica_groups=mesh['angle'=2,'row_0'=32,'row_1'=4,'col'=2] {'row_1'}, use_global_device_ids=true, to_apply=%region_6.7 | all-reduce | flops 1 | bytes 8 | tf_op jit(solution)/shard_map/pmax | solution.py:33
  254.7 16.8 %pmax.23 = f32[]{:T(128)} all-reduce(f32[]{:T(128)} %pmax.22), channel_id=1, replica_groups=mesh['angle'=2,'row_0'=32,'row_1'=4,'col'=2] {'col'}, use_global_device_ids=true, to_apply=%region_7.8 | all-reduce | flops 1 | bytes 8 | tf_op jit(solution)/shard_map/pmax | solution.py:33
  272.2 0.0 copy-start.2
  272.3 0.9 fusion.37
  273.2 546.3 %all-reduce.3.cloned.1.call-done = (f32[2,6,256,256]{3,2,1,0:T(8,128)}, f32[256,256]{1,0:T(8,128)}) async-done(((f32[2,6,256,256]{3,2,1,0:T(8,128)}, f32[256,256]{1,0:T(8,128)}), (f32[2,6,256,256]{3,2,1,0:T(8,128)}, f32[256,256]{1,0:T(8,128)})) %all-reduce.3.cloned.1.call-update) | async-done | bytes 3407888 | tf_op jit(solution)/shard_map/psum | solution.py:149
  819.5 1.6 reduce_max.19
  821.8 1.0 broadcast_add_fusion
  822.7 4.0 divide_add_fusion
  (19 shorter events, 0.3 us)
Async XLA Ops:
  7.2 812.3 %all-reduce.3.cloned.1.call-start = ((), (), s32[]{:S(2)}) async-start(), calls=%async_computation | async-start | bytes 6815744 | tf_op jit(solution)/shard_map/psum | solution.py:149
  7.2 10.5 %collective-permute-start = (f32[2,128,512]{2,1,0:T(8,128)}, f32[2,128,512]{2,1,0:T(8,128)S(1)}, u32[]{:S(2)}, u32[]{:S(2)}) collective-permute-start(f32[2,128,512]{2,1,0:T(8,128)} %param.16), channel_id=1, source_target_pairs={{0,2},{2,4},{4,6},{6,8},{8,10},{10,12},{12,14},{14,16},{16,18},{18... | collective-permute-start | bytes 1572872 | tf_op jit(solution)/shard_map/ppermute | solution.py:24
  11.4 10.2 %collective-permute-start.1 = (f32[2,128,512]{2,1,0:T(8,128)}, f32[2,128,512]{2,1,0:T(8,128)S(1)}, u32[]{:S(2)}, u32[]{:S(2)}) collective-permute-start(f32[2,128,512]{2,1,0:T(8,128)} %param.16), channel_id=1, source_target_pairs={{2,0},{4,2},{6,4},{8,6},{10,8},{12,10},{14,12},{16,14},{18,16},{20... | collective-permute-start | bytes 1572872 | tf_op jit(solution)/shard_map/ppermute | solution.py:27
  18.9 48.4 %copy-start.8 = (s32[1,2]{1,0:T(1,128)S(1)}, s32[1,2]{1,0:T(1,128)}, u32[]{:S(2)}) copy-start(s32[1,2]{1,0:T(1,128)} %param.18) | copy-start | bytes 28
  21.6 1.1 copy-start.3
  23.5 47.3 %collective-permute-start.3 = (f32[2,384,128]{2,1,0:T(8,128)}, f32[2,384,128]{2,1,0:T(8,128)}, u32[]{:S(2)}, u32[]{:S(2)}) collective-permute-start(f32[2,384,128]{2,1,0:T(8,128)} %get-tuple-element.125), channel_id=1, source_target_pairs={{1,0},{3,2},{5,4},{7,6},{9,8},{11,10},{13,12},{15,14},{17,16},{19,... | collective-permute-start | bytes 1179656 | tf_op jit(solution)/shard_map/ppermute | solution.py:27
  66.0 4.8 collective-permute-start.2
  72.4 0.8 copy-start.4
  99.0 3.9 copy-start.7
  148.4 6.1 copy-start
  148.5 6.1 copy-start.1
  150.1 26.7 %collective-permute-start.4 = (f32[3,128,768]{2,1,0:T(8,128)}, f32[3,128,768]{2,1,0:T(8,128)}, u32[]{:S(2)}, u32[]{:S(2)}) collective-permute-start(f32[3,128,768]{2,1,0:T(8,128)} %get-tuple-element.120), channel_id=1, source_target_pairs={{0,2},{2,4},{4,6},{6,8},{8,10},{10,12},{12,14},{14,16},{16,18},{18... | collective-permute-start | bytes 3538952 | tf_op jit(solution)/shard_map/ppermute | solution.py:24
  153.2 28.4 %collective-permute-start.5 = (f32[3,128,768]{2,1,0:T(8,128)}, f32[3,128,768]{2,1,0:T(8,128)}, u32[]{:S(2)}, u32[]{:S(2)}) collective-permute-start(f32[3,128,768]{2,1,0:T(8,128)} %get-tuple-element.121), channel_id=1, source_target_pairs={{2,0},{4,2},{6,4},{8,6},{10,8},{12,10},{14,12},{16,14},{18,16},{20... | collective-permute-start | bytes 3538952 | tf_op jit(solution)/shard_map/ppermute | solution.py:27
  154.6 2.1 copy-start.5
  183.6 88.7 %copy-start.6 = (f32[2,128,512]{2,1,0:T(8,128)S(1)}, f32[2,128,512]{2,1,0:T(8,128)}, u32[]{:S(2)}) copy-start(f32[2,128,512]{2,1,0:T(8,128)} %param.16) | copy-start | bytes 1572868
  183.6 6.0 collective-permute-start.6
  185.1 5.5 collective-permute-start.7
  272.2 550.5 %copy-start.2 = (bf16[2,6,256,256]{3,2,1,0:T(8,128)(2,1)S(1)}, bf16[2,6,256,256]{3,2,1,0:T(8,128)(2,1)}, u32[]{:S(2)}) copy-start(bf16[2,6,256,256]{3,2,1,0:T(8,128)(2,1)} %param.17) | copy-start | bytes 4718596
Sparse Core Ops, SparseCore 0:
  157.6 661.8 all-reduce.2
where the time goes:
time: 845 us; the launch traced here: 834 us
  waiting for transfers between devices  579 us (69%)
  blocking collectives  80.3 us (10%)
  matrix products  62.7 us (7%)
  starting transfers between devices  59.6 us (7%)
  other arithmetic  17.6 us (2%)
  local copies, waits for them, and re-layouts  17.2 us (2%)
  between operations  17.2 us (2%)
    psum x1, waiting for transfers between devices, local(): grad_sum, weight_sum = lax.psum((probe_grad, probe_weight), ROW_COL)  546 us
    pmax x3, blocking collectives, one_axis_at_a_time(): return functools.reduce(lax.pmax, axes, x)  80.3 us
    ppermute x4, starting transfers between devices, padded(): lax.ppermute(lax.slice_in_dim(block, 0, width, axis=dim), axis, backward)  49.5 us
    ppermute x4, waiting for transfers between devices, padded(): lax.ppermute(lax.slice_in_dim(block, block.shape[dim] - width, None, axis...  24.4 us
  transfers between devices with their start and end apart: 9, of which 6 were waited for; matrix products, arithmetic and copies ran while one was open for 1% of the time, Pallas kernels for 0%

commit v1 on v0

v1 whole, which is shorter than its diff:
```python
import functools
import math

import jax
import jax.numpy as jnp
import numpy as np
from jax import lax
from jax.experimental import pallas as pl
from jax.experimental.pallas import tpu as pltpu
from jax.sharding import Mesh
from jax.sharding import PartitionSpec as P

ROW = ("row_0", "row_1")
ANGLE_ROW = ("angle", "row_0", "row_1")
ANGLE_ROW_COL = ("angle", "row_0", "row_1", "col")
VMEM_LIMIT = 60 * 1024 * 1024
ORDER = ((0, 1, 2, 3), False, (0, 3, 5))
MESHID = pl.DeviceIdType.MESH
LANES = 128
NEAR = 4


class Exchange:
    def __init__(self, send_sems, recv_sems, first):
        self.send_sems, self.recv_sems, self.next = send_sems, recv_sems, first
        self.copies = []

    def send(self, src, dst, peer):
        copy = pltpu.make_async_remote_copy(
            src_ref=src,
            dst_ref=dst,
            send_sem=self.send_sems.at[self.next],
            recv_sem=self.recv_sems.at[self.next],
            device_id=peer,
            device_id_type=MESHID,
        )
        copy.start()
        self.next += 1
        self.copies.append(copy)


def rows_at(ref, start, size):
    return ref.at[pl.ds(pl.multiple_of(start, 8), size), :]


def far_order(count):
    return sorted(range(1, count), key=lambda d: -min(d, count - d))


COPIES_PER_CHUNK = 64


def all_sum_kernel(chunks, far, order, x_ref, m_ref, upd_ref, o_ref, om_ref, pair_ref, part_ref, *scratch):
    scratch = list(scratch)
    send_sems, recv_sems = scratch[-2:]
    c, x, z = lax.axis_index("col"), lax.axis_index("row_1"), lax.axis_index("row_0")
    near_at, far_at = lax.rem(z, NEAR), lax.div(z, NEAR)
    partner = {"col": 1 - c}
    x_one = {"row_1": x + 1 - 2 * lax.rem(x, 2)}
    x_two = {"row_1": 3 - x}
    near_peers = {d: {"row_0": far_at * NEAR + lax.rem(near_at + d, NEAR)} for d in range(1, NEAR)}
    far_peers = {d: {"row_0": lax.rem(far_at + d, far) * NEAR + near_at} for d in range(1, far)}
    near_order, far_list = far_order(NEAR), far_order(far)
    barrier = pltpu.get_barrier_semaphore()
    up, down = row_neighbours(x, z, 4, far * NEAR)
    peers = [partner, x_one, x_two, up, down, *near_peers.values(), *far_peers.values()]
    for peer in peers:
        pl.semaphore_signal(barrier, inc=1, device_id=peer, device_id_type=MESHID)
    pl.semaphore_wait(barrier, len(peers))

    mine, theirs = (
        pl.ds(pl.multiple_of(c * LANES, LANES), LANES),
        pl.ds(pl.multiple_of((1 - c) * LANES, LANES), LANES),
    )
    bit_a = lax.rem(lax.div(x + 1, 2), 2)
    bit_b = lax.div(x, 2)
    keep_one, peer_one = (bit_a, bit_b), (x_one, x_two)
    keep_two, peer_two = (bit_b, bit_a), (x_two, x_one)

    class Chunk:
        def __init__(self, index, start, rows, bufs):
            self.start, self.rows, self.bufs = start, rows, bufs
            self.next = index * COPIES_PER_CHUNK
            self.spread = rows // 128 >= 8
            self.pending = None

        def exchange(self):
            self.pending = Exchange(send_sems, recv_sems, self.next)
            return self.pending

        def arrive(self):
            for copy in self.pending.copies:
                copy.wait()
            self.next = self.pending.next

        def step(self, s):
            R, b = self.rows, self.bufs
            if s > 0:
                self.arrive()
            if s == 0:
                e = self.exchange()
                e.send(x_ref.at[pl.ds(self.start, R), theirs], b["rc"], partner)
            elif s == 1:
                b["s0"][...] = x_ref[pl.ds(self.start, R), mine] + b["rc"][...]
                e = self.exchange()
                for h in range(2):
                    src = rows_at(b["s0"], h * (R // 2) + (1 - keep_one[h]) * (R // 4), R // 4)
                    e.send(src, b["r1"].at[h], peer_one[h])
            elif s == 2:
                for h in range(2):
                    kept = pl.ds(pl.multiple_of(h * (R // 2) + keep_one[h] * (R // 4), 8), R // 4)
                    b["s1"][h] = b["s0"][kept, :] + b["r1"][h]
                e = self.exchange()
                for h in range(2):
                    src = rows_at(b["s1"].at[h], (1 - keep_two[h]) * (R // 8), R // 8)
                    e.send(src, b["r2"].at[h], peer_two[h])
            elif s == 3:
                for h in range(2):
                    kept = pl.ds(pl.multiple_of(keep_two[h] * (R // 8), 8), R // 8)
                    b["s2"][pl.ds(h * (R // 8), R // 8), :] = b["s1"][h, kept, :] + b["r2"][h]
                e = self.exchange()
                for d in near_order:
                    src = rows_at(b["s2"], lax.rem(near_at + d, NEAR) * (R // 16), R // 16)
                    e.send(src, b["r3"].at[d - 1], near_peers[d])
            elif s == 4:
                kept = pl.ds(pl.multiple_of(near_at * (R // 16), 8), R // 16)
                total = b["s2"][kept, :]
                for d in range(1, NEAR):
                    total = total + b["r3"][d - 1]
                b["s3"][...] = total
                e = self.exchange()
                for d in far_list:
                    if self.spread:
                        src = rows_at(b["s3"], lax.rem(far_at + d, far) * (R // 128), R // 128)
                    else:
                        src = b["s3"]
                    e.send(src, b["r4"].at[d - 1], far_peers[d])
            elif s == 5:
                if self.spread:
                    at = pl.ds(pl.multiple_of(far_at * (R // 128), 8), R // 128)
                    total = b["s3"][at, :]
                    for d in range(1, far):
                        total = total + b["r4"][d - 1]
                    b["g3"][at, :] = total
                    e = self.exchange()
                    block = rows_at(b["g3"], far_at * (R // 128), R // 128)
                    for d in far_list:
                        e.send(block, block, far_peers[d])
                else:
                    b["r4"][far - 1] = b["s3"][...]
                    total = jnp.zeros((R // 16, LANES), jnp.float32)
                    for owner in range(far):
                        total = total + b["r4"][lax.rem(far_at - owner + far - 1, far)]
                    b["g3"][...] = total
                    self.exchange()
            elif s == 6:
                at = pl.ds(pl.multiple_of(near_at * (R // 16), 8), R // 16)
                e = self.exchange()
                dst = rows_at(b["g2"], near_at * (R // 16), R // 16)
                for d in near_order:
                    e.send(b["g3"], dst, near_peers[d])
                b["g2"][at, :] = b["g3"][...]
            elif s == 7:
                e = self.exchange()
                for h in range(2):
                    src = rows_at(b["g2"], h * (R // 8), R // 8)
                    dst = rows_at(b["g1"].at[h], keep_two[h] * (R // 8), R // 8)
                    e.send(src, dst, peer_two[h])
                for h in range(2):
                    at = pl.ds(pl.multiple_of(keep_two[h] * (R // 8), 8), R // 8)
                    b["g1"][h, at, :] = b["g2"][pl.ds(h * (R // 8), R // 8), :]
            elif s == 8:
                e = self.exchange()
                for h in range(2):
                    dst = rows_at(b["g0"], h * (R // 2) + keep_one[h] * (R // 4), R // 4)
                    e.send(b["g1"].at[h], dst, peer_one[h])
                for h in range(2):
                    at = pl.ds(pl.multiple_of(h * (R // 2) + keep_one[h] * (R // 4), 8), R // 4)
                    b["g0"][at, :] = b["g1"][h]
            elif s == 9:
                e = self.exchange()
                e.send(b["g0"], o_ref.at[pl.ds(self.start, R), mine], partner)
                o_ref[pl.ds(self.start, R), mine] = b["g0"][...]

    class Peak:
        def __init__(self, index, bufs):
            self.next, self.bufs = index * COPIES_PER_CHUNK, bufs
            self.stages = [[partner], [x_one], [x_two], list(near_peers.values()), list(far_peers.values())]
            self.slot = 0
            self.copies = []

        def step(self, s):
            held, came = self.bufs["held"], self.bufs["came"]
            if s > 0:
                top = m_ref[...] if s == 1 else held[s - 1]
                for i, copy in enumerate(self.copies):
                    copy.wait()
                    top = jnp.maximum(top, came[self.slot - len(self.copies) + i])
                if s == 5:
                    om_ref[...] = top
                    return
                held[s] = top
            e = Exchange(send_sems, recv_sems, self.next)
            for peer in self.stages[s]:
                e.send(m_ref if s == 0 else held.at[s], came.at[self.slot], peer)
                self.slot += 1
            self.next, self.copies = e.next, e.copies

    class Fold:
        def __init__(self, index):
            self.index = index

        def step(self, s):
            half = upd_ref.shape[1] // 2
            if s == 0:
                self.first = Exchange(send_sems, recv_sems, self.index * COPIES_PER_CHUNK)
                self.first.send(upd_ref.at[:, pl.ds(half, half), :], part_ref.at[0, c], down)
                self.first.send(upd_ref.at[:, pl.ds(0, half), :], part_ref.at[1, c], up)
                self.first.send(upd_ref, pair_ref, partner)
            elif s == 1:
                self.last = Exchange(send_sems, recv_sems, self.index * COPIES_PER_CHUNK + 8)
                for i in range(2):
                    self.first.copies[i].wait()
                    self.last.send(part_ref.at[i, c], part_ref.at[i, c], partner)
                self.first.copies[2].wait()
            else:
                for copy in self.last.copies:
                    copy.wait()

    fold = Fold(len(chunks) + 1)
    objects = []
    at = 0
    for i, (start, rows) in enumerate(chunks):
        names = chunk_buffers(rows, far)
        bufs = dict(zip(names, scratch[at : at + len(names)]))
        at += len(names)
        objects.append(Chunk(i, start, rows, bufs))
    peak = Peak(len(chunks), dict(held=scratch[at], came=scratch[at + 1]))
    for which, s in order:
        if which == -1:
            peak.step(s)
        elif which == -2:
            fold.step(s)
        else:
            objects[which].step(s)
    for o in objects:
        o.arrive()


def chunk_buffers(rows, far):
    R = rows
    last = R // 128 if R // 128 >= 8 else R // 16
    return dict(
        rc=(R, LANES), s0=(R, LANES), r1=(2, R // 4, LANES), s1=(2, R // 4, LANES), r2=(2, R // 8, LANES),
        s2=(R // 4, LANES), r3=(NEAR - 1, R // 16, LANES), s3=(R // 16, LANES), r4=(far, last, LANES),
        g3=(R // 16, LANES), g2=(R // 4, LANES), g1=(2, R // 4, LANES), g0=(R, LANES),
    )


def wave(count, lags, early, fold_at):
    order = []
    for t in range(10 + max(lags)):
        if t in fold_at:
            order.append((-2, fold_at.index(t)))
        ready = [(i, t - lags[i]) for i in range(count) if 0 <= t - lags[i] < 10]
        order += ready if early else ready[::-1]
        if t < 6:
            order.append((-1, t))
    return order


def all_sum(x, m, upd, far, chunks, order):
    bufs = []
    for _, rows in chunks:
        bufs += [pltpu.VMEM(s, jnp.float32) for s in chunk_buffers(rows, far).values()]
    bufs += [pltpu.VMEM((6, 8, LANES), jnp.float32), pltpu.VMEM((3 + NEAR - 1 + far - 1, 8, LANES), jnp.float32)]
    count = COPIES_PER_CHUNK * (len(chunks) + 2)
    side = upd.shape[1]
    shapes = (x.shape, m.shape, upd.shape, (2, 2, 2, side // 2, side))
    return pl.pallas_call(
        functools.partial(all_sum_kernel, chunks, far, order),
        out_shape=tuple(jax.ShapeDtypeStruct(shape, jnp.float32) for shape in shapes),
        in_specs=[pl.BlockSpec(memory_space=pltpu.VMEM)] * 3,
        out_specs=(pl.BlockSpec(memory_space=pltpu.VMEM),) * 4,
        scratch_shapes=bufs + [pltpu.SemaphoreType.DMA((count,)), pltpu.SemaphoreType.DMA((count,))],
        compiler_params=pltpu.CompilerParams(collective_id=0, has_side_effects=True, vmem_limit_bytes=VMEM_LIMIT),
        name="all_sum",
    )(x, m, upd)


def dft_tables(side):
    half = side // 2
    n, q = np.arange(half)[None, :], np.arange(half)[:, None]
    tables = []
    for odd in range(2):
        phase = 2.0 * np.pi * ((n * (2 * q + odd)) % side) / side
        cosine, sine = np.cos(phase) / math.sqrt(side), np.sin(phase) / math.sqrt(side)
        table = np.block([[cosine, sine], [-sine, cosine]])
        tables += [table, table.T]
    tables = np.stack(tables).astype(np.float32)
    high = tables.astype(jnp.bfloat16)
    low = (tables - high.astype(np.float32)).astype(jnp.bfloat16)
    return np.stack([high, low], axis=1)


def order_table(side):
    table = np.zeros((side, side), np.float32)
    at = np.arange(side)
    table[at, np.where(at < side // 2, 2 * at, 2 * at + 1 - side)] = 1.0
    return table.astype(jnp.bfloat16)


def halves(value):
    high = value.astype(jnp.bfloat16)
    return high, (value - high.astype(jnp.float32)).astype(jnp.bfloat16)


def dot(a, b):
    return jnp.dot(a, b, preferred_element_type=jnp.float32)


def from_left(tab_ref, which, value):
    high, low = halves(value)
    return dot(tab_ref[which, 0], high) + dot(tab_ref[which, 0], low) + dot(tab_ref[which, 1], high)


def from_right(tab_ref, which, value):
    high, low = halves(value)
    return dot(high, tab_ref[which, 0]) + dot(low, tab_ref[which, 0]) + dot(high, tab_ref[which, 1])


def to_far_field(tab_ref, re, im):
    h = re.shape[0] // 2
    plus = jnp.concatenate([re[:h] + re[h:], im[:h] + im[h:]], axis=0)
    minus = jnp.concatenate([re[:h] - re[h:], im[:h] - im[h:]], axis=0)
    even, odd = from_left(tab_ref, 0, plus), from_left(tab_ref, 2, minus)
    re = jnp.concatenate([even[:h], odd[:h]], axis=0)
    im = jnp.concatenate([even[h:], odd[h:]], axis=0)
    plus = jnp.concatenate([re[:, :h] + re[:, h:], im[:, :h] + im[:, h:]], axis=1)
    minus = jnp.concatenate([re[:, :h] - re[:, h:], im[:, :h] - im[:, h:]], axis=1)
    even, odd = from_right(tab_ref, 1, plus), from_right(tab_ref, 3, minus)
    re = jnp.concatenate([even[:, :h], odd[:, :h]], axis=1)
    im = jnp.concatenate([even[:, h:], odd[:, h:]], axis=1)
    return re, im


def from_far_field(tab_ref, re, im):
    h = re.shape[0] // 2
    even = from_right(tab_ref, 0, jnp.concatenate([re[:, :h], im[:, :h]], axis=1))
    odd = from_right(tab_ref, 2, jnp.concatenate([re[:, h:], im[:, h:]], axis=1))
    plus, minus = even + odd, even - odd
    re = jnp.concatenate([plus[:, :h], minus[:, :h]], axis=1)
    im = jnp.concatenate([plus[:, h:], minus[:, h:]], axis=1)
    even = from_left(tab_ref, 1, jnp.concatenate([re[:h], im[:h]], axis=0))
    odd = from_left(tab_ref, 3, jnp.concatenate([re[h:], im[h:]], axis=0))
    plus, minus = even + odd, even - odd
    re = jnp.concatenate([plus[:h], minus[:h]], axis=0)
    im = jnp.concatenate([plus[h:], minus[h:]], axis=0)
    return re, im


def reorder(order_ref, value):
    def three(v):
        high, rest = v.astype(jnp.bfloat16), None
        rest = v - high.astype(jnp.float32)
        middle = rest.astype(jnp.bfloat16)
        return high, middle, (rest - middle.astype(jnp.float32)).astype(jnp.bfloat16)

    table = order_ref[...]
    high, middle, low = three(value)
    value = dot(table, high) + dot(table, middle) + dot(table, low)
    across = lambda v: lax.dot_general(
        v, table, (((1,), (1,)), ((), ())), preferred_element_type=jnp.float32
    )
    high, middle, low = three(value)
    return across(high) + across(middle) + across(low)


def from_row(ref, row, rows, cols):
    off = lax.rem(row, 8)
    value = ref[pl.ds(pl.multiple_of(row - off, 8), rows + 8), cols]
    return pltpu.roll(value, lax.rem(rows + 8 - off, rows + 8), 0)[:rows]


def add_window(acc_ref, source_ref, row, col, scale=None):
    rows = acc_ref.shape[0]
    side = source_ref.shape[1]
    value = from_row(source_ref, row, rows, slice(None))
    if scale is not None:
        value = jnp.where(scale > 0, value, 0.0)
    value = jnp.concatenate([value, jnp.zeros((rows, LANES), jnp.float32)], axis=1)
    value = pltpu.roll(value, lax.rem(col, LANES), 1)
    at = pl.ds(pl.multiple_of(lax.div(col, LANES) * LANES, LANES), side + LANES)
    acc_ref[:, at] = acc_ref[:, at] + value


def sources(cent_ref, tile_cols, margin):
    c = cent_ref[6, 0]
    for where in range(3):
        for side_col in range(2):
            k = where * 2 + side_col
            row = margin - cent_ref[k, 0]
            col = (side_col - c) * tile_cols + cent_ref[k, 1] - margin + tile_cols + margin
            there = jnp.int32(1)
            if where == 0:
                there = cent_ref[7, 0]
            if where == 2:
                there = cent_ref[7, 1]
            yield where, side_col, row, col, there


def wave_kernel(
    cent_ref, ext_ref, probe_ref, amp_ref, tab_ref, order_ref,
    sum_ref, upd_ref, illum_ref, top_ref,
    win, far, amp, acc, shifted,
):
    modes, side = probe_ref.shape[1], probe_ref.shape[2]
    margin = side // 2
    tile_rows, tile_cols = illum_ref.shape
    c = cent_ref[6, 0]
    own_row, own_col = cent_ref[2 + c, 0], cent_ref[2 + c, 1]
    shift = lax.rem(own_col, LANES)
    at = pl.ds(pl.multiple_of(own_col - shift, LANES), side + LANES)
    for p in range(2):
        value = from_row(ext_ref.at[p], own_row, side, at)
        value = pltpu.roll(value, lax.rem(side + LANES - shift, side + LANES), 1)
        win[p] = value[:, :side]
    sum_ref[pl.ds(2 * modes * side, side), :] = win[0] * win[0] + win[1] * win[1]
    shifted[pl.ds(0, side), :] = jnp.zeros((side, side), jnp.float32)
    amp[...] = jnp.zeros_like(amp)

    def forward(m, carry):
        pr, pi = probe_ref[0, m].astype(jnp.float32), probe_ref[1, m].astype(jnp.float32)
        re, im = to_far_field(tab_ref, pr * win[0] - pi * win[1], pr * win[1] + pi * win[0])
        far[m, 0], far[m, 1] = re, im
        amp[...] += re * re + im * im
        shifted[pl.ds(0, side), :] += pr * pr + pi * pi
        return carry

    lax.fori_loop(0, modes, forward, 0)
    amp[...] = reorder(order_ref, amp_ref[0]) / (jnp.sqrt(amp[...]) + 0.5)
    upd_ref[...] = jnp.zeros_like(upd_ref)

    def backward(m, carry):
        factor = amp[...]
        re, im = from_far_field(tab_ref, far[m, 0] * factor, far[m, 1] * factor)
        pr, pi = probe_ref[0, m].astype(jnp.float32), probe_ref[1, m].astype(jnp.float32)
        wr, wi = win[0], win[1]
        re = re - (pr * wr - pi * wi)
        im = im - (pr * wi + pi * wr)
        upd_ref[0] += pr * re + pi * im
        upd_ref[1] += pr * im - pi * re
        at_re, at_im = pl.multiple_of(m * side, 8), pl.multiple_of((modes + m) * side, 8)
        sum_ref[pl.ds(at_re, side), :] = wr * re + wi * im
        sum_ref[pl.ds(at_im, side), :] = wr * im - wi * re
        return carry

    lax.fori_loop(0, modes, backward, 0)

    zeros = jnp.zeros((margin, side), jnp.float32)
    spot_top, spot_bottom = shifted[pl.ds(0, margin), :], shifted[pl.ds(margin, margin), :]
    acc[...] = jnp.zeros_like(acc)
    laid = {0: (spot_bottom, zeros), 1: (spot_top, spot_bottom), 2: (zeros, spot_top)}
    for where, side_col, row, col, there in sources(cent_ref, tile_cols, margin):
        if side_col == 0:
            shifted[pl.ds(0, margin), :], shifted[pl.ds(margin, margin), :] = laid[where]
        add_window(acc, shifted, row, col, there)
    total = acc[:, pl.ds(tile_cols + margin, tile_cols)]
    illum_ref[...] = total
    top_ref[...] = jnp.full(top_ref.shape, jnp.max(total))


def place_kernel(
    cent_ref, obj_ref, probe_ref, upd_ref, pair_ref, part_ref, illum_ref, top_ref, sum_ref,
    new_obj_ref, new_probe_ref, acc, shifted,
):
    modes, side = probe_ref.shape[1], probe_ref.shape[2]
    margin = side // 2
    tile_cols = illum_ref.shape[1]
    c = cent_ref[6, 0]
    below = illum_ref[...] + 0.1 * jnp.max(top_ref[...])
    for p in range(2):
        acc[...] = jnp.zeros_like(acc)
        for where, side_col, row, col, there in sources(cent_ref, tile_cols, margin):
            if where == 1:
                shifted[pl.ds(0, side), :] = jnp.where(c == side_col, upd_ref[p], pair_ref[p])
            else:
                part = part_ref[where // 2, side_col, p]
                first = where // 2 * margin
                shifted[pl.ds(first, margin), :] = part
                shifted[pl.ds(margin - first, margin), :] = jnp.zeros((margin, side), jnp.float32)
            add_window(acc, shifted, row, col, there)
        new_obj_ref[p] = obj_ref[p] + acc[:, pl.ds(tile_cols + margin, tile_cols)] / below
    weight = sum_ref[pl.ds(2 * modes * side, side), :]
    over = weight + 0.1 * jnp.max(weight)

    def finish(m, carry):
        for p in range(2):
            at = pl.ds(pl.multiple_of((p * modes + m) * side, 8), side)
            new_probe_ref[p, m] = probe_ref[p, m].astype(jnp.float32) + sum_ref[at, :] / over
        return carry

    lax.fori_loop(0, modes, finish, 0)


def row_neighbours(x, z, near, deep):
    up = {"row_0": lax.rem(z + deep - (x == 0).astype(jnp.int32), deep), "row_1": lax.rem(x + near - 1, near)}
    down = {"row_0": lax.rem(z + (x == near - 1).astype(jnp.int32), deep), "row_1": lax.rem(x + 1, near)}
    return up, down


def halo_kernel(deep, near, obj_ref, cent_ref, ext_ref, cents_ref, send_sems, recv_sems):
    rows, cols = obj_ref.shape[1], obj_ref.shape[2]
    c, x, z = lax.axis_index("col"), lax.axis_index("row_1"), lax.axis_index("row_0")
    other = {"col": 1 - c}
    up, down = row_neighbours(x, z, near, deep)
    up_other, down_other = dict(up, **other), dict(down, **other)
    barrier = pltpu.get_barrier_semaphore()
    for peer in (other, up, down, up_other, down_other):
        pl.semaphore_signal(barrier, inc=1, device_id=peer, device_id_type=MESHID)
    pl.semaphore_wait(barrier, 5)
    tile = pl.ds(LANES, cols)
    first, last = Exchange(send_sems, recv_sems, 0), Exchange(send_sems, recv_sems, 8)
    edge = pl.ds(pl.multiple_of((1 - c) * (cols - LANES), LANES), LANES)
    held_edge = pl.ds(pl.multiple_of(LANES + (1 - c) * (cols - LANES), LANES), LANES)
    rim = pl.ds(pl.multiple_of(c * (cols + LANES), LANES), LANES)
    first.send(obj_ref, ext_ref.at[:, pl.ds(2 * rows, rows), tile], up)
    first.send(obj_ref, ext_ref.at[:, pl.ds(0, rows), tile], down)
    first.send(obj_ref.at[:, :, edge], ext_ref.at[:, pl.ds(rows, rows), rim], other)
    first.send(cent_ref, cents_ref.at[4 + c], up)
    first.send(cent_ref, cents_ref.at[4 + c], up_other)
    first.send(cent_ref, cents_ref.at[c], down)
    first.send(cent_ref, cents_ref.at[c], down_other)
    first.send(cent_ref, cents_ref.at[2 + c], other)
    cents_ref[2 + c] = cent_ref[...]
    ext_ref[:, pl.ds(rows, rows), tile] = obj_ref[...]
    ext_ref[:, :, rim] = jnp.zeros((2, 3 * rows, LANES), jnp.float32)
    for copy in first.copies[2:]:
        copy.wait()
    for i, start in ((0, 2 * rows), (1, 0)):
        first.copies[i].wait()
        here = pl.ds(start, rows)
        last.send(ext_ref.at[:, here, held_edge], ext_ref.at[:, here, rim], other)
    for copy in last.copies:
        copy.wait()

    @pl.when((x == 0) & (z == 0))
    def _():
        ext_ref[:, pl.ds(0, rows), :] = jnp.zeros((2, rows, cols + 2 * LANES), jnp.float32)

    @pl.when((x == near - 1) & (z == deep - 1))
    def _():
        ext_ref[:, pl.ds(2 * rows, rows), :] = jnp.zeros((2, rows, cols + 2 * LANES), jnp.float32)

def in_vmem(count):
    return [pl.BlockSpec(memory_space=pltpu.VMEM)] * count


def float_shapes(*shapes):
    return tuple(jax.ShapeDtypeStruct(shape, jnp.float32) for shape in shapes)


def local(obj_field, probe_modes, centers, amplitudes):
    _, tile_rows, tile_cols = obj_field.shape
    mode_count, side = probe_modes.shape[1:3]
    deep, near = lax.axis_size("row_0"), lax.axis_size("row_1")
    c, x, z = lax.axis_index("col"), lax.axis_index("row_1"), lax.axis_index("row_0")
    anchor = jnp.stack([(z * near + x) * tile_rows, c * tile_cols])
    cent = jnp.pad(centers - anchor, ((0, 7), (0, LANES - 2)))
    ext, cents = pl.pallas_call(
        functools.partial(halo_kernel, deep, near),
        out_shape=(
            jax.ShapeDtypeStruct((2, 3 * tile_rows, tile_cols + 2 * LANES), jnp.float32),
            jax.ShapeDtypeStruct((6, 8, LANES), jnp.int32),
        ),
        in_specs=in_vmem(2),
        out_specs=tuple(in_vmem(2)),
        scratch_shapes=[pltpu.SemaphoreType.DMA((16,)), pltpu.SemaphoreType.DMA((16,))],
        compiler_params=pltpu.CompilerParams(collective_id=1, has_side_effects=True, vmem_limit_bytes=VMEM_LIMIT),
        name="halo",
    )(obj_field, cent)
    row = z * near + x
    place = jnp.stack([c, c, (row > 0).astype(jnp.int32), (row < deep * near - 1).astype(jnp.int32)])
    cents = jnp.concatenate([cents[:, 0, :2], place.reshape(2, 2)], axis=0)
    planes = 2 * mode_count
    margin = side // 2
    wide = 3 * tile_cols + 2 * LANES
    sums, upd, illumination, top = pl.pallas_call(
        wave_kernel,
        out_shape=float_shapes(
            ((planes + 1) * side, side), (2, side, side), (tile_rows, tile_cols), (8, LANES)
        ),
        in_specs=[pl.BlockSpec(memory_space=pltpu.SMEM)] + in_vmem(5),
        out_specs=tuple(in_vmem(4)),
        scratch_shapes=[
            pltpu.VMEM((2, side, side), jnp.float32),
            pltpu.VMEM((mode_count, 2, side, side), jnp.float32),
            pltpu.VMEM((side, side), jnp.float32),
            pltpu.VMEM((tile_rows, wide), jnp.float32),
            pltpu.VMEM((side + 8, side), jnp.float32),
        ],
        compiler_params=pltpu.CompilerParams(vmem_limit_bytes=VMEM_LIMIT),
        name="waves",
    )(cents, ext, probe_modes, amplitudes, dft_tables(side), order_table(side))
    share = 4 * side
    chunks = ((planes * side, side),) + tuple(
        (start, share) for start in range(0, planes * side, share)
    )
    order = wave(len(chunks), *ORDER)
    sums, top, pair, part = all_sum(sums, top, upd, deep // NEAR, chunks, order)
    return pl.pallas_call(
        place_kernel,
        out_shape=float_shapes(obj_field.shape, probe_modes.shape),
        in_specs=[pl.BlockSpec(memory_space=pltpu.SMEM)] + in_vmem(8),
        out_specs=tuple(in_vmem(2)),
        scratch_shapes=[pltpu.VMEM((tile_rows, wide), jnp.float32), pltpu.VMEM((side + 8, side), jnp.float32)],
        compiler_params=pltpu.CompilerParams(vmem_limit_bytes=VMEM_LIMIT),
        name="place",
    )(cents, obj_field, probe_modes, upd, pair, part, illumination, top, sums)


def solution(mesh):
    split = Mesh(
        mesh.devices.reshape(mesh.shape["angle"], mesh.shape["row"] // 4, 4, mesh.shape["col"]),
        ("angle", "row_0", "row_1", "col"),
    )
    return jax.shard_map(
        local,
        mesh=split,
        in_specs=(
            P(None, ANGLE_ROW, "col"),
            P(),
            P(ANGLE_ROW_COL, None),
            P(ANGLE_ROW_COL, None, None),
        ),
        out_specs=(P(None, ANGLE_ROW, "col"), P(None, "angle", None, None)),
        check_vma=False,
    )
```

time: 845 us -> 200 us (0.24); the launches traced: 834 us -> 199 us
  waiting for transfers between devices: 579 us -> 0 us
  Pallas kernels: 0 us -> 196 us
  blocking collectives: 80.3 us -> 0 us
  matrix products: 62.7 us -> 0 us
  starting transfers between devices: 59.6 us -> 0 us
  between operations: 17.2 us -> 0.66 us
  other arithmetic: 17.6 us -> 1.41 us
  local copies, waits for them, and re-layouts: 17.2 us -> 1.61 us
    psum x1 -> x0, waiting for transfers between devices: 546 us -> none  [local(): grad_sum, weight_sum = lax.psum((probe_grad, probe_weight), ROW_COL)]
    pallas_call x0 -> x4, Pallas kernels: none -> 196 us  [the longest x1 107 us: all_sum(): pl.pallas_call(functools.partial(all_sum_kernel, chunks, far, order), out...]
    pmax x3 -> x0, blocking collectives: 80.3 us -> none  [one_axis_at_a_time(): return functools.reduce(lax.pmax, axes, x)]
    dot_general x16 -> x0, matrix products: 62.7 us -> none  [the longest x2 11.6 us: transform(): jnp.einsum('mkv,lv->mkl', left_real, cosine_table, precision=HIGHEST)]
    ppermute x8 -> x0, starting transfers between devices: 59.5 us -> none  [the longest x4 49.5 us: padded(): lax.ppermute(lax.slice_in_dim(block, 0, width, axis=dim), axis, backward)]
    ppermute x8 -> x0, waiting for transfers between devices: 33 us -> none  [the longest x4 24.4 us: padded(): lax.ppermute(lax.slice_in_dim(block, block.shape[dim] - width, None, axis...]
    dynamic_update_slice x1 -> x0, local copies, waits for them, and re-layouts: 10.7 us -> none  [visit_position(): lax.dynamic_update_slice(buffer, current + stacked, (anchor, start_row, s...]
    add x5 -> x0, other arithmetic: 8.48 us -> none  [the longest x2 4.97 us: local(): new_probe = probe + grad_sum / (weight_sum + 0.1 * peak_weight)]
  transfers between devices with their start and end apart: 9 -> 0, of which waited for: 6 -> 0; matrix products, arithmetic and copies ran while one was open for 1% -> 0% of each run, Pallas kernels for 0% -> 0%
where the time goes in v1:
time: 200 us; the launch traced here: 199 us
  Pallas kernels  196 us (98%)
    pallas_call x1, Pallas kernels, all_sum(): pl.pallas_call(functools.partial(all_sum_kernel, chunks, far, order), out...  107 us
    pallas_call x1, Pallas kernels, local(): pl.pallas_call(functools.partial(halo_kernel, deep, near), out_shape=(jax...  65 us
    pallas_call x1, Pallas kernels, local(): pl.pallas_call(wave_kernel, out_shape=float_shapes(((planes + 1) * side,...  16.7 us
    pallas_call x1, Pallas kernels, local(): pl.pallas_call(place_kernel, out_shape=float_shapes(obj_field.shape, prob...  6.99 us

profile of v1, /device:TPU:33, one launch (start us, length us, event | category | flops | bytes accessed | tf_op | source)
XLA Modules:
  0.0 199.3 jit_solution(12254233410099650272)
XLA Ops:
  0.6 0.1 pad_add_fusion.1
  0.7 0.7 fusion
  1.5 0.1 reshape.7
  1.5 0.6 pad.4.cent_ref
  2.1 65.0 %halo.1 = (f32[2,384,768]{2,1,0:T(8,128)}, s32[6,8,128]{2,1,0:T(8,128)}) custom-call(f32[2,128,512]{2,1,0:T(8,128)} %obj_ref.3, s32[8,128]{1,0:T(8,128)} %pad.4.cent_ref), custom_call_target="tpu_custom_call" | custom-call | tf_op jit(solution)/shard_map/halo/pallas_call | solution.py:570
  67.2 0.7 slice.3
  67.9 0.1 copy.14
  68.0 0.1 copy.15
  68.1 0.6 pad_add_fusion.cent_ref
  68.7 16.7 %waves.1 = (f32[3328,256]{1,0:T(8,128)}, f32[2,256,256]{2,1,0:T(8,128)}, f32[128,512]{1,0:T(8,128)}, f32[8,128]{1,0:T(8,128)}) custom-call(s32[8,2]{1,0:T(8,128)} %pad_add_fusion.cent_ref, f32[2,384,768]{2,1,0:T(8,128)} %get-tuple-element.13.ext_ref, bf16[2,6,256,256]{3,2,1,0:T(8,128)(2,1)} %probe_ref.3, f32[1,256,256]{2,1,0:T(8,128)} %amp_ref.1, ...), custom_call_target="tpu_custom_call" | custom-call | tf_op jit(solution)/shard_map/waves/pallas_call | solution.py:588
  85.4 106.9 %all_sum.1 = (f32[3328,256]{1,0:T(8,128)}, f32[8,128]{1,0:T(8,128)}, f32[2,256,256]{2,1,0:T(8,128)}, f32[2,2,2,128,256]{4,3,2,1,0:T(8,128)}) custom-call(f32[3328,256]{1,0:T(8,128)} %get-tuple-element.15.x_ref, f32[8,128]{1,0:T(8,128)} %get-tuple-element.16.m_ref, f32[2,256,256]{2,1,0:T(8,128)} %get-tuple-element.14.upd_ref), custom_call_target="tpu_custom_call" | custom-call | tf_op jit(solution)/shard_map/all_sum/pallas_call | solution.py:280
  192.3 7.0 %place.1 = (f32[2,128,512]{2,1,0:T(8,128)}, f32[2,6,256,256]{3,2,1,0:T(8,128)}) custom-call(s32[8,2]{1,0:T(8,128)} %pad_add_fusion.cent_ref, f32[2,128,512]{2,1,0:T(8,128)} %obj_ref.3, bf16[2,6,256,256]{3,2,1,0:T(8,128)(2,1)} %probe_ref.3, f32[2,256,256]{2,1,0:T(8,128)} %get-tuple-element.14.upd_ref, f32[2,256,256]{2,1,0:T(8,128)} %get-tuple-element.17.pair_ref, ...), custom_call_target="tpu_custom_call" | custom-call | tf_op jit(solution)/shard_map/place/pallas_call | solution.py:611

commit v2 on v1

--- a/solution.py
+++ b/solution.py
@@ -13,8 +13,16 @@
 ROW = ("row_0", "row_1")
 ANGLE_ROW = ("angle", "row_0", "row_1")
 ANGLE_ROW_COL = ("angle", "row_0", "row_1", "col")
-VMEM_LIMIT = 60 * 1024 * 1024
-ORDER = ((0, 1, 2, 3), False, (0, 3, 5))
+MIB = 1024 * 1024
+BEFORE_BARRIER = (0, 1)
+ORDER = (
+    (0, 0), (-1, 0), (1, 0), (2, 0), (-3, 2), (0, 1), (-1, 1), (1, 1), (2, 1), (3, 0),
+    (0, 2), (-1, 2), (3, 1), (1, 2), (2, 2), (0, 3), (-1, 3), (3, 2), (0, 4), (-1, 4),
+    (1, 3), (2, 3), (3, 3), (-2, 0), (1, 4), (2, 4), (3, 4), (0, 5), (-1, 5), (0, 6),
+    (0, 7), (1, 5), (0, 8), (2, 5), (0, 9), (3, 5), (-2, 1), (1, 6), (2, 6), (1, 7),
+    (3, 6), (2, 7), (1, 8), (3, 7), (2, 8), (1, 9), (3, 8), (2, 9), (3, 9), (-2, 2),
+)
+
 MESHID = pl.DeviceIdType.MESH
 LANES = 128
 NEAR = 4
@@ -50,8 +58,12 @@
 COPIES_PER_CHUNK = 64
 
 
-def all_sum_kernel(chunks, far, order, x_ref, m_ref, upd_ref, o_ref, om_ref, pair_ref, part_ref, *scratch):
+def all_sum_kernel(
+    chunks, far, order, win_ref, probe_ref, amp_ref, tab_ref, order_ref, m_ref,
+    o_ref, om_ref, upd_ref, pair_ref, part_ref, x_ref, waves, factor, *scratch,
+):
     scratch = list(scratch)
+    modes, side = probe_ref.shape[1], probe_ref.shape[2]
     send_sems, recv_sems = scratch[-2:]
     c, x, z = lax.axis_index("col"), lax.axis_index("row_1"), lax.axis_index("row_0")
     near_at, far_at = lax.rem(z, NEAR), lax.div(z, NEAR)
@@ -66,6 +78,16 @@
     peers = [partner, x_one, x_two, up, down, *near_peers.values(), *far_peers.values()]
     for peer in peers:
         pl.semaphore_signal(barrier, inc=1, device_id=peer, device_id_type=MESHID)
+    x_ref[pl.ds(2 * modes * side, side), :] = win_ref[0] * win_ref[0] + win_ref[1] * win_ref[1]
+    upd_ref[...] = jnp.zeros_like(upd_ref)
+    forward_waves(win_ref, probe_ref, amp_ref, tab_ref, order_ref, waves, factor)
+
+    def modes_back(group):
+        per = chunks[1][1] // (2 * side)
+        backward_waves(group * per, per, win_ref, probe_ref, tab_ref, waves, factor, upd_ref, x_ref)
+
+    for group in BEFORE_BARRIER:
+        modes_back(group)
     pl.semaphore_wait(barrier, len(peers))
 
     mine, theirs = (
@@ -241,6 +263,8 @@
             peak.step(s)
         elif which == -2:
             fold.step(s)
+        elif which == -3:
+            modes_back(s)
         else:
             objects[which].step(s)
     for o in objects:
@@ -257,35 +281,29 @@
     )
 
 
-def wave(count, lags, early, fold_at):
-    order = []
-    for t in range(10 + max(lags)):
-        if t in fold_at:
-            order.append((-2, fold_at.index(t)))
-        ready = [(i, t - lags[i]) for i in range(count) if 0 <= t - lags[i] < 10]
-        order += ready if early else ready[::-1]
-        if t < 6:
-            order.append((-1, t))
-    return order
-
-
-def all_sum(x, m, upd, far, chunks, order):
+def all_sum(win, probe, amp, m, far, chunks, order):
     bufs = []
     for _, rows in chunks:
         bufs += [pltpu.VMEM(s, jnp.float32) for s in chunk_buffers(rows, far).values()]
     bufs += [pltpu.VMEM((6, 8, LANES), jnp.float32), pltpu.VMEM((3 + NEAR - 1 + far - 1, 8, LANES), jnp.float32)]
     count = COPIES_PER_CHUNK * (len(chunks) + 2)
-    side = upd.shape[1]
-    shapes = (x.shape, m.shape, upd.shape, (2, 2, 2, side // 2, side))
+    modes, side = probe.shape[1:3]
+    rows = (2 * modes + 1) * side
+    shapes = ((rows, side), m.shape, win.shape, win.shape, (2, 2, 2, side // 2, side))
+    bufs = [
+        pltpu.VMEM((rows, side), jnp.float32),
+        pltpu.VMEM((modes, 2, side, side), jnp.float32),
+        pltpu.VMEM((side, side), jnp.float32),
+    ] + bufs
     return pl.pallas_call(
         functools.partial(all_sum_kernel, chunks, far, order),
         out_shape=tuple(jax.ShapeDtypeStruct(shape, jnp.float32) for shape in shapes),
-        in_specs=[pl.BlockSpec(memory_space=pltpu.VMEM)] * 3,
-        out_specs=(pl.BlockSpec(memory_space=pltpu.VMEM),) * 4,
+        in_specs=[pl.BlockSpec(memory_space=pltpu.VMEM)] * 6,
+        out_specs=(pl.BlockSpec(memory_space=pltpu.VMEM),) * 5,
         scratch_shapes=bufs + [pltpu.SemaphoreType.DMA((count,)), pltpu.SemaphoreType.DMA((count,))],
-        compiler_params=pltpu.CompilerParams(collective_id=0, has_side_effects=True, vmem_limit_bytes=VMEM_LIMIT),
+        compiler_params=pltpu.CompilerParams(collective_id=0, has_side_effects=True, vmem_limit_bytes=30 * MIB),
         name="all_sum",
-    )(x, m, upd)
+    )(win, probe, amp, dft_tables(side), order_table(side), m)
 
 
 def dft_tables(side):
@@ -409,11 +427,41 @@
             yield where, side_col, row, col, there
 
 
-def wave_kernel(
-    cent_ref, ext_ref, probe_ref, amp_ref, tab_ref, order_ref,
-    sum_ref, upd_ref, illum_ref, top_ref,
-    win, far, amp, acc, shifted,
-):
+def forward_waves(win, probe_ref, amp_ref, tab_ref, order_ref, far, amp):
+    amp[...] = jnp.zeros_like(amp)
+
+    def forward(m, carry):
+        pr, pi = probe_ref[0, m].astype(jnp.float32), probe_ref[1, m].astype(jnp.float32)
+        re, im = to_far_field(tab_ref, pr * win[0] - pi * win[1], pr * win[1] + pi * win[0])
+        far[m, 0], far[m, 1] = re, im
+        amp[...] += re * re + im * im
+        return carry
+
+    lax.fori_loop(0, probe_ref.shape[1], forward, 0)
+    amp[...] = reorder(order_ref, amp_ref[0]) / (jnp.sqrt(amp[...]) + 0.5)
+
+
+def backward_waves(first, count, win, probe_ref, tab_ref, far, amp, upd_ref, sum_ref):
+    side = probe_ref.shape[2]
+
+    def backward(m, carry):
+        factor = amp[...]
+        re, im = from_far_field(tab_ref, far[m, 0] * factor, far[m, 1] * factor)
+        pr, pi = probe_ref[0, m].astype(jnp.float32), probe_ref[1, m].astype(jnp.float32)
+        wr, wi = win[0], win[1]
+        re = re - (pr * wr - pi * wi)
+        im = im - (pr * wi + pi * wr)
+        upd_ref[0] += pr * re + pi * im
+        upd_ref[1] += pr * im - pi * re
+        at_re, at_im = pl.multiple_of(2 * m * side, 8), pl.multiple_of((2 * m + 1) * side, 8)
+        sum_ref[pl.ds(at_re, side), :] = wr * re + wi * im
+        sum_ref[pl.ds(at_im, side), :] = wr * im - wi * re
+        return carry
+
+    lax.fori_loop(first, first + count, backward, 0)
+
+
+def window_kernel(cent_ref, ext_ref, probe_ref, win_ref, illum_ref, top_ref, acc, shifted):
     modes, side = probe_ref.shape[1], probe_ref.shape[2]
     margin = side // 2
     tile_rows, tile_cols = illum_ref.shape
@@ -424,39 +472,12 @@
     for p in range(2):
         value = from_row(ext_ref.at[p], own_row, side, at)
         value = pltpu.roll(value, lax.rem(side + LANES - shift, side + LANES), 1)
-        win[p] = value[:, :side]
-    sum_ref[pl.ds(2 * modes * side, side), :] = win[0] * win[0] + win[1] * win[1]
-    shifted[pl.ds(0, side), :] = jnp.zeros((side, side), jnp.float32)
-    amp[...] = jnp.zeros_like(amp)
-
-    def forward(m, carry):
+        win_ref[p] = value[:, :side]
+    spot = jnp.zeros((side, side), jnp.float32)
+    for m in range(modes):
         pr, pi = probe_ref[0, m].astype(jnp.float32), probe_ref[1, m].astype(jnp.float32)
-        re, im = to_far_field(tab_ref, pr * win[0] - pi * win[1], pr * win[1] + pi * win[0])
-        far[m, 0], far[m, 1] = re, im
-        amp[...] += re * re + im * im
-        shifted[pl.ds(0, side), :] += pr * pr + pi * pi
-        return carry
-
-    lax.fori_loop(0, modes, forward, 0)
-    amp[...] = reorder(order_ref, amp_ref[0]) / (jnp.sqrt(amp[...]) + 0.5)
-    upd_ref[...] = jnp.zeros_like(upd_ref)
-
-    def backward(m, carry):
-        factor = amp[...]
-        re, im = from_far_field(tab_ref, far[m, 0] * factor, far[m, 1] * factor)
-        pr, pi = probe_ref[0, m].astype(jnp.float32), probe_ref[1, m].astype(jnp.float32)
-        wr, wi = win[0], win[1]
-        re = re - (pr * wr - pi * wi)
-        im = im - (pr * wi + pi * wr)
-        upd_ref[0] += pr * re + pi * im
-        upd_ref[1] += pr * im - pi * re
-        at_re, at_im = pl.multiple_of(m * side, 8), pl.multiple_of((modes + m) * side, 8)
-        sum_ref[pl.ds(at_re, side), :] = wr * re + wi * im
-        sum_ref[pl.ds(at_im, side), :] = wr * im - wi * re
-        return carry
-
-    lax.fori_loop(0, modes, backward, 0)
-
+        spot = spot + (pr * pr + pi * pi)
+    shifted[pl.ds(0, side), :] = spot
     zeros = jnp.zeros((margin, side), jnp.float32)
     spot_top, spot_bottom = shifted[pl.ds(0, margin), :], shifted[pl.ds(margin, margin), :]
     acc[...] = jnp.zeros_like(acc)
@@ -496,7 +517,7 @@
 
     def finish(m, carry):
         for p in range(2):
-            at = pl.ds(pl.multiple_of((p * modes + m) * side, 8), side)
+            at = pl.ds(pl.multiple_of((2 * m + p) * side, 8), side)
             new_probe_ref[p, m] = probe_ref[p, m].astype(jnp.float32) + sum_ref[at, :] / over
         return carry
 
@@ -576,7 +597,7 @@
         in_specs=in_vmem(2),
         out_specs=tuple(in_vmem(2)),
         scratch_shapes=[pltpu.SemaphoreType.DMA((16,)), pltpu.SemaphoreType.DMA((16,))],
-        compiler_params=pltpu.CompilerParams(collective_id=1, has_side_effects=True, vmem_limit_bytes=VMEM_LIMIT),
+        compiler_params=pltpu.CompilerParams(collective_id=1, has_side_effects=True, vmem_limit_bytes=6 * MIB),
         name="halo",
     )(obj_field, cent)
     row = z * near + x
@@ -585,36 +606,27 @@
     planes = 2 * mode_count
     margin = side // 2
     wide = 3 * tile_cols + 2 * LANES
-    sums, upd, illumination, top = pl.pallas_call(
-        wave_kernel,
-        out_shape=float_shapes(
-            ((planes + 1) * side, side), (2, side, side), (tile_rows, tile_cols), (8, LANES)
-        ),
-        in_specs=[pl.BlockSpec(memory_space=pltpu.SMEM)] + in_vmem(5),
-        out_specs=tuple(in_vmem(4)),
-        scratch_shapes=[
-            pltpu.VMEM((2, side, side), jnp.float32),
-            pltpu.VMEM((mode_count, 2, side, side), jnp.float32),
-            pltpu.VMEM((side, side), jnp.float32),
-            pltpu.VMEM((tile_rows, wide), jnp.float32),
-            pltpu.VMEM((side + 8, side), jnp.float32),
-        ],
-        compiler_params=pltpu.CompilerParams(vmem_limit_bytes=VMEM_LIMIT),
-        name="waves",
-    )(cents, ext, probe_modes, amplitudes, dft_tables(side), order_table(side))
+    win, illumination, top = pl.pallas_call(
+        window_kernel,
+        out_shape=float_shapes((2, side, side), (tile_rows, tile_cols), (8, LANES)),
+        in_specs=[pl.BlockSpec(memory_space=pltpu.SMEM)] + in_vmem(2),
+        out_specs=tuple(in_vmem(3)),
+        scratch_shapes=[pltpu.VMEM((tile_rows, wide), jnp.float32), pltpu.VMEM((side + 8, side), jnp.float32)],
+        compiler_params=pltpu.CompilerParams(vmem_limit_bytes=8 * MIB),
+        name="window",
+    )(cents, ext, probe_modes)
     share = 4 * side
     chunks = ((planes * side, side),) + tuple(
         (start, share) for start in range(0, planes * side, share)
     )
-    order = wave(len(chunks), *ORDER)
-    sums, top, pair, part = all_sum(sums, top, upd, deep // NEAR, chunks, order)
+    sums, top, upd, pair, part = all_sum(win, probe_modes, amplitudes, top, deep // NEAR, chunks, ORDER)
     return pl.pallas_call(
         place_kernel,
         out_shape=float_shapes(obj_field.shape, probe_modes.shape),
         in_specs=[pl.BlockSpec(memory_space=pltpu.SMEM)] + in_vmem(8),
         out_specs=tuple(in_vmem(2)),
         scratch_shapes=[pltpu.VMEM((tile_rows, wide), jnp.float32), pltpu.VMEM((side + 8, side), jnp.float32)],
-        compiler_params=pltpu.CompilerParams(vmem_limit_bytes=VMEM_LIMIT),
+        compiler_params=pltpu.CompilerParams(vmem_limit_bytes=16 * MIB),
         name="place",
     )(cents, obj_field, probe_modes, upd, pair, part, illumination, top, sums)
 

time: 200 us -> 177 us (0.89)
  Pallas kernels: 196 us -> 172 us
    pallas_call x1, Pallas kernels: 16.7 us -> 2.09 us  [local(): pl.pallas_call(window_kernel, out_shape=float_shapes((2, side, side), (ti...]
    pallas_call x1, Pallas kernels: 107 us -> 103 us  [all_sum(): pl.pallas_call(functools.partial(all_sum_kernel, chunks, far, order), out...]
    pallas_call x1, Pallas kernels: 6.99 us -> 4.23 us  [local(): pl.pallas_call(place_kernel, out_shape=float_shapes(obj_field.shape, prob...]
    unnamed x0 -> x14, local copies, waits for them, and re-layouts: none -> 2.46 us
    pallas_call x1, Pallas kernels: 65 us -> 62.8 us  [local(): pl.pallas_call(functools.partial(halo_kernel, deep, near), out_shape=(jax...]
where the time goes in v2:
time: 177 us; the launch traced here: 176 us
  Pallas kernels  172 us (97%)
  local copies, waits for them, and re-layouts  2.74 us (2%)
    pallas_call x1, Pallas kernels, all_sum(): pl.pallas_call(functools.partial(all_sum_kernel, chunks, far, order), out...  103 us
    pallas_call x1, Pallas kernels, local(): pl.pallas_call(functools.partial(halo_kernel, deep, near), out_shape=(jax...  62.8 us
    pallas_call x1, Pallas kernels, local(): pl.pallas_call(place_kernel, out_shape=float_shapes(obj_field.shape, prob...  4.23 us

profile of v2, /device:TPU:33, one launch (start us, length us, event | category | flops | bytes accessed | tf_op | source)
XLA Modules:
  0.0 176.4 jit_solution(5959779335310850236)
XLA Ops:
  0.6 0.1 pad_add_fusion.1
  0.7 0.7 fusion
  1.5 0.1 reshape.7
  1.5 0.0 copy-start.2
  1.5 1.0 copy-done.2
  2.6 0.0 copy-start.5
  2.6 0.0 copy-start.6
  2.6 62.8 %halo.1 = (f32[2,384,768]{2,1,0:T(8,128)S(1)}, s32[6,8,128]{2,1,0:T(8,128)S(1)}) custom-call(f32[2,128,512]{2,1,0:T(8,128)S(1)} %copy-done.2, s32[8,128]{1,0:T(8,128)S(1)} %pad.4.cent_ref), custom_call_target="tpu_custom_call" | custom-call | tf_op jit(solution)/shard_map/halo/pallas_call | solution.py:591
  65.4 0.1 copy.14
  65.5 0.1 copy.15
  65.6 0.0 copy-start
  65.6 1.4 copy-done
  67.0 0.0 copy-start.1
  67.0 0.0 copy-start.4
  67.0 0.0 copy-start.3
  67.0 2.1 %window.1 = (f32[2,256,256]{2,1,0:T(8,128)S(1)}, f32[128,512]{1,0:T(8,128)S(1)}, f32[8,128]{1,0:T(8,128)S(1)}) custom-call(s32[8,2]{1,0:T(8,128)S(1)} %pad_add_fusion.cent_ref, f32[2,384,768]{2,1,0:T(8,128)S(1)} %get-tuple-element.13.ext_ref, bf16[2,6,256,256]{3,2,1,0:T(8,128)(2,1)S(1)} %copy-done), custom_call_target="tpu_custom_call" | custom-call | tf_op jit(solution)/shard_map/window/pallas_call | solution.py:609
  69.1 0.0 copy-done.5
  69.1 0.0 copy-done.6
  69.1 0.0 copy-done.1
  69.1 0.0 copy-done.4
  69.1 103.1 %all_sum.1 = (f32[3328,256]{1,0:T(8,128)S(1)}, f32[8,128]{1,0:T(8,128)S(1)}, f32[2,256,256]{2,1,0:T(8,128)S(1)}, f32[2,256,256]{2,1,0:T(8,128)S(1)}, f32[2,2,2,128,256]{4,3,2,1,0:T(8,128)S(1)}) custom-call(f32[2,256,256]{2,1,0:T(8,128)S(1)} %get-tuple-element.14.win_ref, bf16[2,6,256,256]{3,2,1,0:T(8,128)(2,1)S(1)} %copy-done.1, ...), custom_call_target="tpu_custom_call" | custom-call | tf_op jit(solution)/shard_map/all_sum/pallas_call | solution.py:298
  172.2 0.0 copy-done.3
  172.2 4.2 %place.1 = (f32[2,128,512]{2,1,0:T(8,128)}, f32[2,6,256,256]{3,2,1,0:T(8,128)}) custom-call(s32[8,2]{1,0:T(8,128)S(1)} %pad_add_fusion.cent_ref, f32[2,128,512]{2,1,0:T(8,128)S(1)} %copy-done.3, bf16[2,6,256,256]{3,2,1,0:T(8,128)(2,1)S(1)} %copy-done.1, f32[2,256,256]{2,1,0:T(8,128)S(1)} %get-tuple-element.16.upd_ref, ...), custom_call_target="tpu_custom_call" | custom-call | tf_op jit(solution)/shard_map/place/pallas_call | solution.py:623
  (3 shorter events, 0.0 us)
Async XLA Ops:
  1.5 1.0 copy-start.2
  2.6 66.5 %copy-start.5 = (f32[1,256,256]{2,1,0:T(8,128)S(1)}, f32[1,256,256]{2,1,0:T(8,128)}, u32[]{:S(2)}) copy-start(f32[1,256,256]{2,1,0:T(8,128)} %amp_ref.1) | copy-start | bytes 786436
  2.6 66.5 %copy-start.6 = (bf16[256,256]{1,0:T(8,128)(2,1)S(1)}, bf16[256,256]{1,0:T(8,128)(2,1)}, u32[]{:S(2)}) copy-start(bf16[256,256]{1,0:T(8,128)(2,1)} %constant.28.clone.order_ref) | copy-start | bytes 393220
  65.6 1.4 copy-start
  67.0 2.1 %copy-start.1 = (bf16[2,6,256,256]{3,2,1,0:T(8,128)(2,1)S(1)}, bf16[2,6,256,256]{3,2,1,0:T(8,128)(2,1)}, u32[]{:S(2)}) copy-start(bf16[2,6,256,256]{3,2,1,0:T(8,128)(2,1)} %probe_ref.5) | copy-start | bytes 4718596
  67.0 2.1 %copy-start.4 = (bf16[4,2,256,256]{3,2,1,0:T(8,128)(2,1)S(1)}, bf16[4,2,256,256]{3,2,1,0:T(8,128)(2,1)}, u32[]{:S(2)}) copy-start(bf16[4,2,256,256]{3,2,1,0:T(8,128)(2,1)} %constant.27.clone.tab_ref) | copy-start | bytes 3145732
  67.0 105.2 %copy-start.3 = (f32[2,128,512]{2,1,0:T(8,128)S(1)}, f32[2,128,512]{2,1,0:T(8,128)}, u32[]{:S(2)}) copy-start(f32[2,128,512]{2,1,0:T(8,128)} %obj_ref.3) | copy-start | bytes 1572868

commit v3 on v2

--- a/solution.py
+++ b/solution.py
@@ -16,11 +16,12 @@
 MIB = 1024 * 1024
 BEFORE_BARRIER = (0, 1)
 ORDER = (
-    (0, 0), (-1, 0), (1, 0), (2, 0), (-3, 2), (0, 1), (-1, 1), (1, 1), (2, 1), (3, 0),
-    (0, 2), (-1, 2), (3, 1), (1, 2), (2, 2), (0, 3), (-1, 3), (3, 2), (0, 4), (-1, 4),
-    (1, 3), (2, 3), (3, 3), (-2, 0), (1, 4), (2, 4), (3, 4), (0, 5), (-1, 5), (0, 6),
-    (0, 7), (1, 5), (0, 8), (2, 5), (0, 9), (3, 5), (-2, 1), (1, 6), (2, 6), (1, 7),
-    (3, 6), (2, 7), (1, 8), (3, 7), (2, 8), (1, 9), (3, 8), (2, 9), (3, 9), (-2, 2),
+    (1, 0), (2, 0), (1, 1), (2, 1), (-3, 2), (3, 0), (0, 0), (-1, 0), (1, 2), (3, 1),
+    (2, 2), (1, 3), (0, 1), (-1, 1), (3, 2), (1, 4), (2, 3), (0, 2), (-1, 2), (3, 3),
+    (2, 4), (0, 3), (-1, 3), (1, 5), (0, 4), (-1, 4), (-2, 0), (3, 4), (2, 5), (3, 5),
+    (0, 5), (-1, 5), (1, 6), (2, 6), (-2, 1), (3, 6), (0, 6), (-1, 6), (1, 7), (1, 8),
+    (2, 7), (1, 9), (3, 7), (2, 8), (1, 10), (0, 7), (3, 8), (2, 9), (0, 8), (3, 9),
+    (0, 9), (2, 10), (1, 11), (-2, 2), (3, 10), (2, 11), (0, 10), (3, 11), (0, 11),
 )
 
 MESHID = pl.DeviceIdType.MESH
@@ -66,16 +67,26 @@
     modes, side = probe_ref.shape[1], probe_ref.shape[2]
     send_sems, recv_sems = scratch[-2:]
     c, x, z = lax.axis_index("col"), lax.axis_index("row_1"), lax.axis_index("row_0")
-    near_at, far_at = lax.rem(z, NEAR), lax.div(z, NEAR)
+    far_at, deep = lax.div(z, NEAR), far * NEAR
     partner = {"col": 1 - c}
     x_one = {"row_1": x + 1 - 2 * lax.rem(x, 2)}
     x_two = {"row_1": 3 - x}
-    near_peers = {d: {"row_0": far_at * NEAR + lax.rem(near_at + d, NEAR)} for d in range(1, NEAR)}
-    far_peers = {d: {"row_0": lax.rem(far_at + d, far) * NEAR + near_at} for d in range(1, far)}
-    near_order, far_list = far_order(NEAR), far_order(far)
+    bit_a = lax.rem(lax.div(x + 1, 2), 2)
+    bit_b = lax.div(x, 2)
+    halvings = [((x_one, bit_a), (x_two, bit_b)), ((x_two, bit_b), (x_one, bit_a))]
+    for reach in (1, 2):
+        pairs = []
+        for shift in (0, NEAR - 1):
+            at = lax.rem(z + shift, NEAR)
+            bit = lax.rem(lax.div(at, reach), 2)
+            pairs.append(({"row_0": lax.rem(z + deep + reach - 2 * reach * bit, deep)}, bit))
+        halvings.append(tuple(pairs))
+    near_peers = [peer for level in halvings[2:] for peer, _ in level]
+    far_peers = {d: {"row_0": lax.rem(far_at + d, far) * NEAR + lax.rem(z, NEAR)} for d in range(1, far)}
+    far_list = far_order(far)
     barrier = pltpu.get_barrier_semaphore()
-    up, down = row_neighbours(x, z, 4, far * NEAR)
-    peers = [partner, x_one, x_two, up, down, *near_peers.values(), *far_peers.values()]
+    up, down = row_neighbours(x, z, 4, deep)
+    peers = [partner, x_one, x_two, up, down, *near_peers, *far_peers.values()]
     for peer in peers:
         pl.semaphore_signal(barrier, inc=1, device_id=peer, device_id_type=MESHID)
     x_ref[pl.ds(2 * modes * side, side), :] = win_ref[0] * win_ref[0] + win_ref[1] * win_ref[1]
@@ -94,16 +105,12 @@
         pl.ds(pl.multiple_of(c * LANES, LANES), LANES),
         pl.ds(pl.multiple_of((1 - c) * LANES, LANES), LANES),
     )
-    bit_a = lax.rem(lax.div(x + 1, 2), 2)
-    bit_b = lax.div(x, 2)
-    keep_one, peer_one = (bit_a, bit_b), (x_one, x_two)
-    keep_two, peer_two = (bit_b, bit_a), (x_two, x_one)
 
     class Chunk:
         def __init__(self, index, start, rows, bufs):
             self.start, self.rows, self.bufs = start, rows, bufs
             self.next = index * COPIES_PER_CHUNK
-            self.spread = rows // 128 >= 8
+            self.whole = rows // 128 >= 8
             self.pending = None
 
         def exchange(self):
@@ -115,99 +122,80 @@
                 copy.wait()
             self.next = self.pending.next
 
+        def held(self, name, level, h):
+            ref = self.bufs[name + str(level)]
+            return ref.at[pl.ds(h * (self.rows // 2), self.rows // 2), :] if level == 0 else ref.at[h]
+
+        def tile_of(self, name, owner):
+            half_group = far // 2
+            first = lax.rem(owner, half_group) * 8 if self.whole else 0
+            return self.bufs[name].at[lax.div(owner, half_group)].at[pl.ds(pl.multiple_of(first, 8), 8), :]
+
         def step(self, s):
-            R, b = self.rows, self.bufs
+            R, b, steps = self.rows, self.bufs, len(halvings)
             if s > 0:
                 self.arrive()
+            e = self.exchange()
             if s == 0:
-                e = self.exchange()
                 e.send(x_ref.at[pl.ds(self.start, R), theirs], b["rc"], partner)
-            elif s == 1:
-                b["s0"][...] = x_ref[pl.ds(self.start, R), mine] + b["rc"][...]
-                e = self.exchange()
+            elif s <= steps:
+                level = s - 1
+                if level == 0:
+                    b["s0"][...] = x_ref[pl.ds(self.start, R), mine] + b["rc"][...]
+                else:
+                    self.add(level)
+                size = R >> (level + 2)
                 for h in range(2):
-                    src = rows_at(b["s0"], h * (R // 2) + (1 - keep_one[h]) * (R // 4), R // 4)
-                    e.send(src, b["r1"].at[h], peer_one[h])
-            elif s == 2:
-                for h in range(2):
-                    kept = pl.ds(pl.multiple_of(h * (R // 2) + keep_one[h] * (R // 4), 8), R // 4)
-                    b["s1"][h] = b["s0"][kept, :] + b["r1"][h]
-                e = self.exchange()
-                for h in range(2):
-                    src = rows_at(b["s1"].at[h], (1 - keep_two[h]) * (R // 8), R // 8)
-                    e.send(src, b["r2"].at[h], peer_two[h])
-            elif s == 3:
-                for h in range(2):
-                    kept = pl.ds(pl.multiple_of(keep_two[h] * (R // 8), 8), R // 8)
-                    b["s2"][pl.ds(h * (R // 8), R // 8), :] = b["s1"][h, kept, :] + b["r2"][h]
-                e = self.exchange()
-                for d in near_order:
-                    src = rows_at(b["s2"], lax.rem(near_at + d, NEAR) * (R // 16), R // 16)
-                    e.send(src, b["r3"].at[d - 1], near_peers[d])
-            elif s == 4:
-                kept = pl.ds(pl.multiple_of(near_at * (R // 16), 8), R // 16)
-                total = b["s2"][kept, :]
-                for d in range(1, NEAR):
-                    total = total + b["r3"][d - 1]
-                b["s3"][...] = total
-                e = self.exchange()
+                    peer, keep = halvings[level][h]
+                    e.send(rows_at(self.held("s", level, h), (1 - keep) * size, size), b["r" + str(level)].at[h], peer)
+            elif s == steps + 1:
+                self.add(steps)
                 for d in far_list:
-                    if self.spread:
-                        src = rows_at(b["s3"], lax.rem(far_at + d, far) * (R // 128), R // 128)
-                    else:
-                        src = b["s3"]
-                    e.send(src, b["r4"].at[d - 1], far_peers[d])
-            elif s == 5:
-                if self.spread:
-                    at = pl.ds(pl.multiple_of(far_at * (R // 128), 8), R // 128)
-                    total = b["s3"][at, :]
+                    src = self.tile_of("s" + str(steps), lax.rem(far_at + d, far))
+                    e.send(src, b["rf"].at[d - 1], far_peers[d])
+            elif s == steps + 2:
+                own = self.tile_of("s" + str(steps), far_at)
+                block = self.tile_of("g" + str(steps), far_at)
+                if self.whole:
+                    total = own[...]
                     for d in range(1, far):
-                        total = total + b["r4"][d - 1]
-                    b["g3"][at, :] = total
-                    e = self.exchange()
-                    block = rows_at(b["g3"], far_at * (R // 128), R // 128)
+                        total = total + b["rf"][d - 1]
+                    block[...] = total
                     for d in far_list:
                         e.send(block, block, far_peers[d])
                 else:
-                    b["r4"][far - 1] = b["s3"][...]
-                    total = jnp.zeros((R // 16, LANES), jnp.float32)
+                    b["rf"][far - 1] = own[...]
+                    total = jnp.zeros((8, LANES), jnp.float32)
                     for owner in range(far):
-                        total = total + b["r4"][lax.rem(far_at - owner + far - 1, far)]
-                    b["g3"][...] = total
-                    self.exchange()
-            elif s == 6:
-                at = pl.ds(pl.multiple_of(near_at * (R // 16), 8), R // 16)
-                e = self.exchange()
-                dst = rows_at(b["g2"], near_at * (R // 16), R // 16)
-                for d in near_order:
-                    e.send(b["g3"], dst, near_peers[d])
-                b["g2"][at, :] = b["g3"][...]
-            elif s == 7:
-                e = self.exchange()
+                        total = total + b["rf"][lax.rem(far_at - owner + far - 1 + far, far)]
+                    block[...] = total
+                    e.send(block, block, far_peers[far // 2])
+            elif s <= 2 * steps + 2:
+                level = 2 * steps + 2 - s
+                size = R >> (level + 2)
                 for h in range(2):
-                    src = rows_at(b["g2"], h * (R // 8), R // 8)
-                    dst = rows_at(b["g1"].at[h], keep_two[h] * (R // 8), R // 8)
-                    e.send(src, dst, peer_two[h])
+                    peer, keep = halvings[level][h]
+                    target = rows_at(self.held("g", level, h), keep * size, size)
+                    e.send(self.held("g", level + 1, h), target, peer)
                 for h in range(2):
-                    at = pl.ds(pl.multiple_of(keep_two[h] * (R // 8), 8), R // 8)
-                    b["g1"][h, at, :] = b["g2"][pl.ds(h * (R // 8), R // 8), :]
-            elif s == 8:
-                e = self.exchange()
-                for h in range(2):
-                    dst = rows_at(b["g0"], h * (R // 2) + keep_one[h] * (R // 4), R // 4)
-                    e.send(b["g1"].at[h], dst, peer_one[h])
-                for h in range(2):
-                    at = pl.ds(pl.multiple_of(h * (R // 2) + keep_one[h] * (R // 4), 8), R // 4)
-                    b["g0"][at, :] = b["g1"][h]
-            elif s == 9:
-                e = self.exchange()
+                    _, keep = halvings[level][h]
+                    target = rows_at(self.held("g", level, h), keep * size, size)
+                    target[...] = self.held("g", level + 1, h)[...]
+            else:
                 e.send(b["g0"], o_ref.at[pl.ds(self.start, R), mine], partner)
                 o_ref[pl.ds(self.start, R), mine] = b["g0"][...]
+
+        def add(self, level):
+            size = self.rows >> (level + 1)
+            for h in range(2):
+                _, keep = halvings[level - 1][h]
+                kept = rows_at(self.held("s", level - 1, h), keep * size, size)
+                self.bufs["s" + str(level)][h] = kept[...] + self.bufs["r" + str(level - 1)][h]
 
     class Peak:
         def __init__(self, index, bufs):
             self.next, self.bufs = index * COPIES_PER_CHUNK, bufs
-            self.stages = [[partner], [x_one], [x_two], list(near_peers.values()), list(far_peers.values())]
+            self.stages = [[partner], *[[level[0][0]] for level in halvings], list(far_peers.values())]
             self.slot = 0
             self.copies = []
 
@@ -218,7 +206,7 @@
                 for i, copy in enumerate(self.copies):
                     copy.wait()
                     top = jnp.maximum(top, came[self.slot - len(self.copies) + i])
-                if s == 5:
+                if s == len(self.stages):
                     om_ref[...] = top
                     return
                 held[s] = top
@@ -272,20 +260,19 @@
 
 
 def chunk_buffers(rows, far):
-    R = rows
-    last = R // 128 if R // 128 >= 8 else R // 16
-    return dict(
-        rc=(R, LANES), s0=(R, LANES), r1=(2, R // 4, LANES), s1=(2, R // 4, LANES), r2=(2, R // 8, LANES),
-        s2=(R // 4, LANES), r3=(NEAR - 1, R // 16, LANES), s3=(R // 16, LANES), r4=(far, last, LANES),
-        g3=(R // 16, LANES), g2=(R // 4, LANES), g1=(2, R // 4, LANES), g0=(R, LANES),
-    )
+    steps = 4
+    shapes = dict(rc=(rows, LANES), s0=(rows, LANES), g0=(rows, LANES), rf=(far, 8, LANES))
+    for level in range(1, steps + 1):
+        size = rows >> (level + 1)
+        shapes["r" + str(level - 1)] = shapes["s" + str(level)] = shapes["g" + str(level)] = (2, size, LANES)
+    return shapes
 
 
 def all_sum(win, probe, amp, m, far, chunks, order):
     bufs = []
     for _, rows in chunks:
         bufs += [pltpu.VMEM(s, jnp.float32) for s in chunk_buffers(rows, far).values()]
-    bufs += [pltpu.VMEM((6, 8, LANES), jnp.float32), pltpu.VMEM((3 + NEAR - 1 + far - 1, 8, LANES), jnp.float32)]
+    bufs += [pltpu.VMEM((6, 8, LANES), jnp.float32), pltpu.VMEM((5 + far - 1, 8, LANES), jnp.float32)]
     count = COPIES_PER_CHUNK * (len(chunks) + 2)
     modes, side = probe.shape[1:3]
     rows = (2 * modes + 1) * side

time: 177 us -> 182 us (1.028)
  Pallas kernels: 172 us -> 178 us
    pallas_call x1, Pallas kernels: 103 us -> 108 us  [all_sum(): pl.pallas_call(functools.partial(all_sum_kernel, chunks, far, order), out...]
where the time goes in v3:
time: 182 us
  Pallas kernels  178 us (98%)
  local copies, waits for them, and re-layouts  2.74 us (2%)
    pallas_call x1, Pallas kernels, all_sum(): pl.pallas_call(functools.partial(all_sum_kernel, chunks, far, order), out...  108 us
    pallas_call x1, Pallas kernels, local(): pl.pallas_call(functools.partial(halo_kernel, deep, near), out_shape=(jax...  62.8 us
    pallas_call x1, Pallas kernels, local(): pl.pallas_call(place_kernel, out_shape=float_shapes(obj_field.shape, prob...  4.23 us

profile of v3, /device:TPU:33, one launch (start us, length us, event | category | flops | bytes accessed | tf_op | source)
XLA Modules:
  0.0 181.8 jit_solution(10998382441165427943)
XLA Ops:
  0.6 0.1 pad_add_fusion.1
  0.7 0.7 fusion
  1.5 0.1 reshape.7
  1.5 0.0 copy-start.2
  1.5 1.0 copy-done.2
  2.6 0.0 copy-start.5
  2.6 0.0 copy-start.6
  2.6 62.8 %halo.1 = (f32[2,384,768]{2,1,0:T(8,128)S(1)}, s32[6,8,128]{2,1,0:T(8,128)S(1)}) custom-call(f32[2,128,512]{2,1,0:T(8,128)S(1)} %copy-done.2, s32[8,128]{1,0:T(8,128)S(1)} %pad.4.cent_ref), custom_call_target="tpu_custom_call" | custom-call | tf_op jit(solution)/shard_map/halo/pallas_call | solution.py:578
  65.4 0.1 copy.14
  65.5 0.1 copy.15
  65.6 0.0 copy-start
  65.6 1.4 copy-done
  67.0 0.0 copy-start.1
  67.0 0.0 copy-start.4
  67.0 0.0 copy-start.3
  67.0 2.1 %window.1 = (f32[2,256,256]{2,1,0:T(8,128)S(1)}, f32[128,512]{1,0:T(8,128)S(1)}, f32[8,128]{1,0:T(8,128)S(1)}) custom-call(s32[8,2]{1,0:T(8,128)S(1)} %pad_add_fusion.cent_ref, f32[2,384,768]{2,1,0:T(8,128)S(1)} %get-tuple-element.13.ext_ref, bf16[2,6,256,256]{3,2,1,0:T(8,128)(2,1)S(1)} %copy-done), custom_call_target="tpu_custom_call" | custom-call | tf_op jit(solution)/shard_map/window/pallas_call | solution.py:596
  69.1 0.0 copy-done.5
  69.1 0.0 copy-done.6
  69.1 0.0 copy-done.1
  69.1 0.0 copy-done.4
  69.1 108.5 %all_sum.1 = (f32[3328,256]{1,0:T(8,128)S(1)}, f32[8,128]{1,0:T(8,128)S(1)}, f32[2,256,256]{2,1,0:T(8,128)S(1)}, f32[2,256,256]{2,1,0:T(8,128)S(1)}, f32[2,2,2,128,256]{4,3,2,1,0:T(8,128)S(1)}) custom-call(f32[2,256,256]{2,1,0:T(8,128)S(1)} %get-tuple-element.14.win_ref, bf16[2,6,256,256]{3,2,1,0:T(8,128)(2,1)S(1)} %copy-done.1, ...), custom_call_target="tpu_custom_call" | custom-call | tf_op jit(solution)/shard_map/all_sum/pallas_call | solution.py:285
  177.6 0.0 copy-done.3
  177.6 4.2 %place.1 = (f32[2,128,512]{2,1,0:T(8,128)}, f32[2,6,256,256]{3,2,1,0:T(8,128)}) custom-call(s32[8,2]{1,0:T(8,128)S(1)} %pad_add_fusion.cent_ref, f32[2,128,512]{2,1,0:T(8,128)S(1)} %copy-done.3, bf16[2,6,256,256]{3,2,1,0:T(8,128)(2,1)S(1)} %copy-done.1, f32[2,256,256]{2,1,0:T(8,128)S(1)} %get-tuple-element.16.upd_ref, ...), custom_call_target="tpu_custom_call" | custom-call | tf_op jit(solution)/shard_map/place/pallas_call | solution.py:610
  (3 shorter events, 0.0 us)
Async XLA Ops:
  1.5 1.0 copy-start.2
  2.6 66.5 %copy-start.5 = (f32[1,256,256]{2,1,0:T(8,128)S(1)}, f32[1,256,256]{2,1,0:T(8,128)}, u32[]{:S(2)}) copy-start(f32[1,256,256]{2,1,0:T(8,128)} %amp_ref.1) | copy-start | bytes 786436
  2.6 66.5 %copy-start.6 = (bf16[256,256]{1,0:T(8,128)(2,1)S(1)}, bf16[256,256]{1,0:T(8,128)(2,1)}, u32[]{:S(2)}) copy-start(bf16[256,256]{1,0:T(8,128)(2,1)} %constant.28.clone.order_ref) | copy-start | bytes 393220
  65.6 1.4 copy-start
  67.0 2.1 %copy-start.1 = (bf16[2,6,256,256]{3,2,1,0:T(8,128)(2,1)S(1)}, bf16[2,6,256,256]{3,2,1,0:T(8,128)(2,1)}, u32[]{:S(2)}) copy-start(bf16[2,6,256,256]{3,2,1,0:T(8,128)(2,1)} %probe_ref.5) | copy-start | bytes 4718596
  67.0 2.1 %copy-start.4 = (bf16[4,2,256,256]{3,2,1,0:T(8,128)(2,1)S(1)}, bf16[4,2,256,256]{3,2,1,0:T(8,128)(2,1)}, u32[]{:S(2)}) copy-start(bf16[4,2,256,256]{3,2,1,0:T(8,128)(2,1)} %constant.27.clone.tab_ref) | copy-start | bytes 3145732
  67.0 110.6 %copy-start.3 = (f32[2,128,512]{2,1,0:T(8,128)S(1)}, f32[2,128,512]{2,1,0:T(8,128)}, u32[]{:S(2)}) copy-start(f32[2,128,512]{2,1,0:T(8,128)} %obj_ref.3) | copy-start | bytes 1572868

commit v4 on v2

--- a/solution.py
+++ b/solution.py
@@ -16,11 +16,11 @@
 MIB = 1024 * 1024
 BEFORE_BARRIER = (0, 1)
 ORDER = (
-    (0, 0), (-1, 0), (1, 0), (2, 0), (-3, 2), (0, 1), (-1, 1), (1, 1), (2, 1), (3, 0),
-    (0, 2), (-1, 2), (3, 1), (1, 2), (2, 2), (0, 3), (-1, 3), (3, 2), (0, 4), (-1, 4),
-    (1, 3), (2, 3), (3, 3), (-2, 0), (1, 4), (2, 4), (3, 4), (0, 5), (-1, 5), (0, 6),
-    (0, 7), (1, 5), (0, 8), (2, 5), (0, 9), (3, 5), (-2, 1), (1, 6), (2, 6), (1, 7),
-    (3, 6), (2, 7), (1, 8), (3, 7), (2, 8), (1, 9), (3, 8), (2, 9), (3, 9), (-2, 2),
+    (0, 0), (-1, 0), (1, 0), (2, 0), (-3, 2), (3, 0), (0, 1), (-1, 1), (1, 1), (2, 1),
+    (3, 1), (0, 2), (-1, 2), (1, 2), (2, 2), (3, 2), (0, 3), (-1, 3), (1, 3), (2, 3),
+    (3, 3), (0, 4), (-1, 4), (1, 4), (2, 4), (3, 4), (-2, 0), (0, 5), (-1, 5), (1, 5),
+    (2, 5), (3, 5), (0, 6), (1, 6), (2, 6), (3, 6), (-2, 1), (0, 7), (1, 7), (2, 7),
+    (3, 7), (0, 8), (1, 8), (2, 8), (3, 8), (0, 9), (1, 9), (2, 9), (3, 9), (-2, 2),
 )
 
 MESHID = pl.DeviceIdType.MESH

time: 177 us -> 172 us (0.972)
  Pallas kernels: 172 us -> 167 us
    pallas_call x1, Pallas kernels: 103 us -> 98.2 us  [all_sum(): pl.pallas_call(functools.partial(all_sum_kernel, chunks, far, order), out...]
where the time goes in v4:
time: 172 us
  Pallas kernels  167 us (97%)
  local copies, waits for them, and re-layouts  2.74 us (2%)
    pallas_call x1, Pallas kernels, all_sum(): pl.pallas_call(functools.partial(all_sum_kernel, chunks, far, order), out...  98.2 us
    pallas_call x1, Pallas kernels, local(): pl.pallas_call(functools.partial(halo_kernel, deep, near), out_shape=(jax...  62.8 us
    pallas_call x1, Pallas kernels, local(): pl.pallas_call(place_kernel, out_shape=float_shapes(obj_field.shape, prob...  4.23 us

profile of v4, /device:TPU:33, one launch (start us, length us, event | category | flops | bytes accessed | tf_op | source)
XLA Modules:
  0.0 171.5 jit_solution(155490549464031061)
XLA Ops:
  0.6 0.1 pad_add_fusion.1
  0.7 0.7 fusion
  1.5 0.1 reshape.7
  1.5 0.0 copy-start.2
  1.5 1.0 copy-done.2
  2.6 0.0 copy-start.5
  2.6 0.0 copy-start.6
  2.6 62.8 %halo.1 = (f32[2,384,768]{2,1,0:T(8,128)S(1)}, s32[6,8,128]{2,1,0:T(8,128)S(1)}) custom-call(f32[2,128,512]{2,1,0:T(8,128)S(1)} %copy-done.2, s32[8,128]{1,0:T(8,128)S(1)} %pad.4.cent_ref), custom_call_target="tpu_custom_call" | custom-call | tf_op jit(solution)/shard_map/halo/pallas_call | solution.py:591
  65.4 0.1 copy.14
  65.5 0.1 copy.15
  65.6 0.0 copy-start
  65.6 1.4 copy-done
  67.0 0.0 copy-start.1
  67.0 0.0 copy-start.4
  67.0 0.0 copy-start.3
  67.0 2.1 %window.1 = (f32[2,256,256]{2,1,0:T(8,128)S(1)}, f32[128,512]{1,0:T(8,128)S(1)}, f32[8,128]{1,0:T(8,128)S(1)}) custom-call(s32[8,2]{1,0:T(8,128)S(1)} %pad_add_fusion.cent_ref, f32[2,384,768]{2,1,0:T(8,128)S(1)} %get-tuple-element.13.ext_ref, bf16[2,6,256,256]{3,2,1,0:T(8,128)(2,1)S(1)} %copy-done), custom_call_target="tpu_custom_call" | custom-call | tf_op jit(solution)/shard_map/window/pallas_call | solution.py:609
  69.1 0.0 copy-done.5
  69.1 0.0 copy-done.6
  69.1 0.0 copy-done.1
  69.1 0.0 copy-done.4
  69.1 98.2 %all_sum.1 = (f32[3328,256]{1,0:T(8,128)S(1)}, f32[8,128]{1,0:T(8,128)S(1)}, f32[2,256,256]{2,1,0:T(8,128)S(1)}, f32[2,256,256]{2,1,0:T(8,128)S(1)}, f32[2,2,2,128,256]{4,3,2,1,0:T(8,128)S(1)}) custom-call(f32[2,256,256]{2,1,0:T(8,128)S(1)} %get-tuple-element.14.win_ref, bf16[2,6,256,256]{3,2,1,0:T(8,128)(2,1)S(1)} %copy-done.1, ...), custom_call_target="tpu_custom_call" | custom-call | tf_op jit(solution)/shard_map/all_sum/pallas_call | solution.py:298
  167.3 0.0 copy-done.3
  167.3 4.2 %place.1 = (f32[2,128,512]{2,1,0:T(8,128)}, f32[2,6,256,256]{3,2,1,0:T(8,128)}) custom-call(s32[8,2]{1,0:T(8,128)S(1)} %pad_add_fusion.cent_ref, f32[2,128,512]{2,1,0:T(8,128)S(1)} %copy-done.3, bf16[2,6,256,256]{3,2,1,0:T(8,128)(2,1)S(1)} %copy-done.1, f32[2,256,256]{2,1,0:T(8,128)S(1)} %get-tuple-element.16.upd_ref, ...), custom_call_target="tpu_custom_call" | custom-call | tf_op jit(solution)/shard_map/place/pallas_call | solution.py:623
  (3 shorter events, 0.0 us)
Async XLA Ops:
  1.5 1.0 copy-start.2
  2.6 66.5 %copy-start.5 = (f32[1,256,256]{2,1,0:T(8,128)S(1)}, f32[1,256,256]{2,1,0:T(8,128)}, u32[]{:S(2)}) copy-start(f32[1,256,256]{2,1,0:T(8,128)} %amp_ref.1) | copy-start | bytes 786436
  2.6 66.5 %copy-start.6 = (bf16[256,256]{1,0:T(8,128)(2,1)S(1)}, bf16[256,256]{1,0:T(8,128)(2,1)}, u32[]{:S(2)}) copy-start(bf16[256,256]{1,0:T(8,128)(2,1)} %constant.28.clone.order_ref) | copy-start | bytes 393220
  65.6 1.4 copy-start
  67.0 2.1 %copy-start.1 = (bf16[2,6,256,256]{3,2,1,0:T(8,128)(2,1)S(1)}, bf16[2,6,256,256]{3,2,1,0:T(8,128)(2,1)}, u32[]{:S(2)}) copy-start(bf16[2,6,256,256]{3,2,1,0:T(8,128)(2,1)} %probe_ref.5) | copy-start | bytes 4718596
  67.0 2.1 %copy-start.4 = (bf16[4,2,256,256]{3,2,1,0:T(8,128)(2,1)S(1)}, bf16[4,2,256,256]{3,2,1,0:T(8,128)(2,1)}, u32[]{:S(2)}) copy-start(bf16[4,2,256,256]{3,2,1,0:T(8,128)(2,1)} %constant.27.clone.tab_ref) | copy-start | bytes 3145732
  67.0 100.3 %copy-start.3 = (f32[2,128,512]{2,1,0:T(8,128)S(1)}, f32[2,128,512]{2,1,0:T(8,128)}, u32[]{:S(2)}) copy-start(f32[2,128,512]{2,1,0:T(8,128)} %obj_ref.3) | copy-start | bytes 1572868
